TPU v7x, 128 devices: a whole 4x4x4 slice. The times are simulated.
128 devices in a mesh: gx: 4 (over y), gy: 8 (over z, core), gz: 4 (over x).
Axes of the slice: x: 4, y: 4, z: 4, core: 2. Of those that a mesh axis runs over, the one named last changes fastest.
Arguments:
- params: float32 [12, 7168, 1536], P('gx', 'gy', 'gz'), may hold values from -100 to 100
- grads: bfloat16 [12, 7168, 1536], P('gx', 'gy', 'gz'), may hold values from -300 to 300
- row_state: float32 [12, 7168], P('gx', 'gy'), may hold values from 0.01 to 1
- col_state: float32 [12, 1536], P('gx', 'gz'), may hold values from 0.01 to 1
Outputs:
- new_params: float32 [12, 7168, 1536], P('gx', 'gy', 'gz')
- row_new: float32 [12, 7168], P('gx', 'gy')
- col_new: float32 [12, 1536], P('gx', 'gz')
- applied_step: float32 [12, 7168, 1536], P('gx', 'gy', 'gz')
- compute_copy: bfloat16 [12, 7168, 1536], P('gx', 'gy')
All inputs are finite; a program needn't handle non-finite values.
Results may differ from a plain program's by a relative error of at most 0.0004.
Values may be sent and summed in bfloat16 or wider, within the bound.
A program may use at most 128 MiB of HBM per device.

v0:
```python
import jax
import jax.numpy as jnp
from jax import lax
from jax.sharding import Mesh
from jax.sharding import PartitionSpec as P

GY = ("gy_0", "gy_1")
GY_GZ = ("gy_0", "gy_1", "gz")
GX_GY_GZ = ("gx", "gy_0", "gy_1", "gz")


decay_rate = 0.842
tiny_term = 1e-30
step_share = 0.01
clip_limit = 1.0


def copy_for_each(x, axis):
    length = lax.axis_size(axis)
    return lax.all_to_all(jnp.broadcast_to(x[None], (length, *x.shape)), axis, 0, 0, tiled=True)


def of_everyone(x, axis):
    everything = copy_for_each(x, axis)
    return jnp.sum(everything, axis=0)


def by_axis(x, axes):
    for axis in axes:
        x = lax.psum(x, axis)
    return x


def factor_stats(weights, gradient, row_old, col_old):
    grad_float = gradient.astype(jnp.float32)
    squares = grad_float * grad_float + tiny_term
    columns = gradient.shape[2] * lax.axis_size("gz")
    rows_all = gradient.shape[1] * lax.axis_size(GY)
    row_sum = of_everyone(jnp.sum(squares, axis=2), "gz")
    col_sum = of_everyone(jnp.sum(squares, axis=1), GY)
    row_new = decay_rate * row_old + (1.0 - decay_rate) * (row_sum / columns)
    col_new = decay_rate * col_old + (1.0 - decay_rate) * (col_sum / rows_all)
    weight_sq = jnp.sum(weights * weights, axis=(1, 2))
    weight_total = of_everyone(weight_sq, GY_GZ)
    row_total = of_everyone(jnp.sum(row_new, axis=1), GY)
    row_norm = row_new / (row_total / rows_all)[:, None]
    update = grad_float * lax.rsqrt(row_norm[:, :, None] * col_new[:, None, :])
    update_sq = jnp.sum(update * update, axis=(1, 2))
    weight_scale = jnp.sqrt(weight_total / (rows_all * columns))
    return (update, update_sq, weight_scale, row_new, col_new)


def gather_copy(halves):
    return lax.all_gather(halves, "gz", axis=2, tiled=True)


def body(params, grads, row_state, col_state):
    update, update_sq, weight_scale, row_new, col_new = factor_stats(
        params, grads, row_state, col_state
    )
    update_total = by_axis(jnp.sum(update_sq), GX_GY_GZ)
    entries = params.size * lax.axis_size("gx") * lax.axis_size(GY) * lax.axis_size("gz")
    root_mean = jnp.sqrt(update_total / entries)
    clip_factor = jnp.maximum(1.0, root_mean / clip_limit)
    applied = weight_scale[:, None, None] * update / clip_factor
    new_params = params - step_share * applied
    copy_half = new_params.astype(jnp.bfloat16)
    compute = gather_copy(copy_half)
    return (new_params, row_new, col_new, applied, compute)


def solution(mesh):
    split = Mesh(
        mesh.devices.reshape(mesh.shape["gx"], 4, 2, mesh.shape["gz"]), ("gx", "gy_0", "gy_1", "gz")
    )
    placed = (P("gx", GY, "gz"), P("gx", GY, "gz"), P("gx", GY), P("gx", "gz"))
    return jax.shard_map(
        body,
        mesh=split,
        in_specs=placed,
        out_specs=(
            P("gx", GY, "gz"),
            P("gx", GY),
            P("gx", "gz"),
            P("gx", GY, "gz"),
            P("gx", GY, None),
        ),
        check_vma=False,
    )
```

profile of v0, /device:TPU:1, one launch (start us, length us, event | category | flops | bytes accessed | tf_op | source)
XLA Modules:
  0.0 182.9 jit_solution(2472894583006311007)
XLA Ops:
  7.2 0.0 copy-start
  7.2 0.0 copy-start.3
  7.2 0.0 copy-start.4
  7.2 2.5 %fusion.2 = (f32[3,896]{1,0:T(4,128)S(1)}, f32[3,384]{1,0:T(4,128)S(1)}) fusion(bf16[3,896,384]{2,1,0:T(8,128)(2,1)} %param.5), kind=kLoop, calls=%fused_computation.4 | loop fusion | flops 5157120 | bytes 2079744 | tf_op jit(solution)/shard_map/reduce_sum | solution.py:39
  9.7 0.6 broadcast_in_dim.9
  10.3 4.8 %all-to-all-start.1 = ((f32[4,3,896]{2,1,0:T(4,128)}), f32[4,3,896]{2,1,0:T(4,128)S(1)}, u32[]{:S(2)}, u32[]{:S(2)}) async-start(f32[4,3,896]{2,1,0:T(4,128)} %broadcast_in_dim.9), calls=%async_computation.1 | async-start | bytes 114688 | tf_op jit(solution)/shard_map/all_to_all | solution.py:20
  15.2 2.6 %multiply_reduce_fusion.1 = f32[3]{0:T(128)S(1)} fusion(f32[3,896,384]{2,1,0:T(8,128)} %param.4), kind=kLoop, calls=%fused_computation.8 | loop fusion | flops 2064381 | bytes 4128780 | tf_op jit(solution)/shard_map/reduce_sum | solution.py:43
  17.8 1.8 all-to-all-done.1
  19.6 0.6 broadcast_in_dim.11
  20.2 7.4 %all-to-all-start.3 = ((f32[8,3,384]{2,1,0:T(4,128)}), f32[8,3,384]{2,1,0:T(4,128)S(1)}, u32[]{:S(2)}, u32[]{:S(2)}) async-start(f32[8,3,384]{2,1,0:T(4,128)} %broadcast_in_dim.11), calls=%async_computation.3 | async-start | bytes 98304 | tf_op jit(solution)/shard_map/all_to_all | solution.py:20
  27.7 0.1 fusion.4
  27.8 4.6 %all-to-all-done.3 = f32[8,3,384]{2,1,0:T(4,128)S(1)} async-done(((f32[8,3,384]{2,1,0:T(4,128)}), f32[8,3,384]{2,1,0:T(4,128)S(1)}, u32[]{:S(2)}, u32[]{:S(2)}) %all-to-all-start.3) | async-done | bytes 36896 | tf_op jit(solution)/shard_map/all_to_all | solution.py:20
  32.4 0.6 broadcast_in_dim.10
  33.0 4.0 %all-to-all-start.2 = ((f32[8,1,3]{2,1,0:T(1,128)}), f32[8,1,3]{2,1,0:T(1,128)S(1)}, u32[]{:S(2)}, u32[]{:S(2)}) async-start(f32[8,1,3]{2,1,0:T(1,128)} %broadcast_in_dim.10), calls=%async_computation.2 | async-start | bytes 8192 | tf_op jit(solution)/shard_map/all_to_all | solution.py:20
  37.0 0.0 copy-start.2
  37.0 4.5 %all-to-all-done.2 = f32[8,1,3]{2,1,0:T(1,128)S(1)} async-done(((f32[8,1,3]{2,1,0:T(1,128)}), f32[8,1,3]{2,1,0:T(1,128)S(1)}, u32[]{:S(2)}, u32[]{:S(2)}) %all-to-all-start.2) | async-done | bytes 128 | tf_op jit(solution)/shard_map/all_to_all | solution.py:20
  41.5 0.6 broadcast_in_dim.8
  42.2 4.2 %all-to-all-start = ((f32[32,1,3]{2,1,0:T(1,128)}), f32[32,1,3]{2,1,0:T(1,128)S(1)}, u32[]{:S(2)}, u32[]{:S(2)}) async-start(f32[32,1,3]{2,1,0:T(1,128)} %broadcast_in_dim.8), calls=%async_computation | async-start | bytes 32768 | tf_op jit(solution)/shard_map/all_to_all | solution.py:20
  46.4 0.0 all-gather.2.cloned.1.call-start
  46.4 0.1 broadcast_divide_fusion
  46.5 2.2 %multiply_reduce_fusion = f32[]{:T(128)} fusion(bf16[3,896,384]{2,1,0:T(8,128)(2,1)S(1)} %copy-done, f32[3,384]{1,0:T(4,128)S(1)} %multiply_add_fusion.1, f32[3,896]{1,0:T(4,128)S(1)} %broadcast_divide_fusion), kind=kLoop, calls=%fused_computation.6 | loop fusion | flops 5160959 | bytes 2079748 | tf_op jit(solution)/shard_map/reduce_sum | solution.py:61
  48.7 9.3 %psum.28 = f32[]{:T(128)} all-reduce(f32[]{:T(128)} %multiply_reduce_fusion), channel_id=1, replica_groups=mesh['gx'=4,'gy_0'=4,'gy_1'=2,'gz'=4] {'gx'}, use_global_device_ids=true, to_apply=%region_9.0 | all-reduce | flops 1 | bytes 8 | tf_op jit(solution)/shard_map/psum | solution.py:30
  58.0 9.3 %psum.29 = f32[]{:T(128)} all-reduce(f32[]{:T(128)} %psum.28), channel_id=1, replica_groups=mesh['gx'=4,'gy_0'=4,'gy_1'=2,'gz'=4] {'gy_0'}, use_global_device_ids=true, to_apply=%region_10.0 | all-reduce | flops 1 | bytes 8 | tf_op jit(solution)/shard_map/psum | solution.py:30
  67.4 0.0 all-to-all-done
  67.4 0.1 reduce_sum.86
  67.4 7.2 %psum.30 = f32[]{:T(128)} all-reduce(f32[]{:T(128)} %psum.29), channel_id=1, replica_groups=mesh['gx'=4,'gy_0'=4,'gy_1'=2,'gz'=4] {'gy_1'}, use_global_device_ids=true, to_apply=%region_11.0 | all-reduce | flops 1 | bytes 8 | tf_op jit(solution)/shard_map/psum | solution.py:30
  74.6 9.0 %psum.31 = f32[]{:T(128)} all-reduce(f32[]{:T(128)} %psum.30), channel_id=1, replica_groups=mesh['gx'=4,'gy_0'=4,'gy_1'=2,'gz'=4] {'gz'}, use_global_device_ids=true, to_apply=%region_12.0 | all-reduce | flops 1 | bytes 8 | tf_op jit(solution)/shard_map/psum | solution.py:30
  84.3 6.2 %fusion.3 = (bf16[3,896,384]{2,1,0:T(8,128)(2,1)}, f32[3,896,384]{2,1,0:T(8,128)}, f32[3,896,384]{2,1,0:T(8,128)}) fusion(f32[3,896,384]{2,1,0:T(8,128)} %param.4, f32[]{:T(128)S(6)} %max.3, f32[3,384]{1,0:T(4,128)S(1)} %multiply_add_fusion.1, f32[3,896]{1,0:T(4,128)S(1)} %broadcast_divide_fusion, bf16[3,896,384]{2,1,0:T(8,128)(2,1)S(1)} %copy-done, ...), kind=kLoop, calls=%fused_computation.14 | loop fusion | flops 8257536 | bytes 16530448 | tf_op jit(solution)/shard_map/convert_element_type | solution.py:67
  90.5 0.0 copy-done.2
  90.5 0.0 all-gather.2.cloned.1.call-update
  90.5 78.3 %all-gather.2.cloned.1.call-done = bf16[3,896,1536]{2,1,0:T(8,128)(2,1)} async-done(((bf16[3,896,384]{2,1,0:T(8,128)(2,1)}), bf16[3,896,1536]{2,1,0:T(8,128)(2,1)}) %all-gather.2.cloned.1.call-update) | async-done | bytes 8257552 | tf_op jit(solution)/shard_map/all_gather | solution.py:54
  168.8 7.2 %copy.22 = bf16[3,896,1536]{2,1,0:T(8,128)(2,1)} copy(bf16[3,896,1536]{2,1,0:T(8,128)(2,1)} %all-gather.2.cloned.1.call-done) | data formatting | bytes 16515072
  (11 shorter events, 0.1 us)
Async XLA Ops:
  7.2 39.4 %copy-start = (bf16[3,896,384]{2,1,0:T(8,128)(2,1)S(1)}, bf16[3,896,384]{2,1,0:T(8,128)(2,1)}, u32[]{:S(2)}) copy-start(bf16[3,896,384]{2,1,0:T(8,128)(2,1)} %param.5) | copy-start | bytes 6193156
  7.2 20.5 %copy-start.3 = (f32[3,896]{1,0:T(4,128)S(1)}, f32[3,896]{1,0:T(4,128)}, u32[]{:S(2)}) copy-start(f32[3,896]{1,0:T(4,128)} %param.6) | copy-start | bytes 32260
  7.2 29.8 %copy-start.4 = (f32[3,384]{1,0:T(4,128)S(1)}, f32[3,384]{1,0:T(4,128)}, u32[]{:S(2)}) copy-start(f32[3,384]{1,0:T(4,128)} %param.7) | copy-start | bytes 13828
  10.3 9.3 %all-to-all-start.1 = ((f32[4,3,896]{2,1,0:T(4,128)}), f32[4,3,896]{2,1,0:T(4,128)S(1)}, u32[]{:S(2)}, u32[]{:S(2)}) async-start(f32[4,3,896]{2,1,0:T(4,128)} %broadcast_in_dim.9), calls=%async_computation.1 | async-start | bytes 114688 | tf_op jit(solution)/shard_map/all_to_all | solution.py:20
  20.2 12.2 %all-to-all-start.3 = ((f32[8,3,384]{2,1,0:T(4,128)}), f32[8,3,384]{2,1,0:T(4,128)S(1)}, u32[]{:S(2)}, u32[]{:S(2)}) async-start(f32[8,3,384]{2,1,0:T(4,128)} %broadcast_in_dim.11), calls=%async_computation.3 | async-start | bytes 98304 | tf_op jit(solution)/shard_map/all_to_all | solution.py:20
  27.8 62.7 %copy-start.1 = (f32[3,896]{1,0:T(4,128)}, f32[3,896]{1,0:T(4,128)S(1)}, u32[]{:S(2)}) copy-start(f32[3,896]{1,0:T(4,128)S(1)} %get-tuple-element.18) | copy-start | bytes 32260
  33.0 8.5 %all-to-all-start.2 = ((f32[8,1,3]{2,1,0:T(1,128)}), f32[8,1,3]{2,1,0:T(1,128)S(1)}, u32[]{:S(2)}, u32[]{:S(2)}) async-start(f32[8,1,3]{2,1,0:T(1,128)} %broadcast_in_dim.10), calls=%async_computation.2 | async-start | bytes 8192 | tf_op jit(solution)/shard_map/all_to_all | solution.py:20
  37.0 53.4 %copy-start.2 = (f32[3,384]{1,0:T(4,128)}, f32[3,384]{1,0:T(4,128)S(1)}, u32[]{:S(2)}) copy-start(f32[3,384]{1,0:T(4,128)S(1)} %multiply_add_fusion.1) | copy-start | bytes 13828
  42.2 25.2 %all-to-all-start = ((f32[32,1,3]{2,1,0:T(1,128)}), f32[32,1,3]{2,1,0:T(1,128)S(1)}, u32[]{:S(2)}, u32[]{:S(2)}) async-start(f32[32,1,3]{2,1,0:T(1,128)} %broadcast_in_dim.8), calls=%async_computation | async-start | bytes 32768 | tf_op jit(solution)/shard_map/all_to_all | solution.py:20
  46.4 122.4 %all-gather.2.cloned.1.call-start = ((), (), s32[]{:S(2)}) async-start(), calls=%async_computation.4 | async-start | bytes 10321920 | tf_op jit(solution)/shard_map/all_gather | solution.py:54
Sparse Core Ops, SparseCore 0:
  90.6 78.1 all-gather.1
where the time goes:
time: 183 us
  waiting for transfers between devices  89.2 us (49%)
  blocking collectives  34.8 us (19%)
  starting transfers between devices  20.4 us (11%)
  between operations  14.8 us (8%)
  other arithmetic  13.8 us (8%)
  local copies, waits for them, and re-layouts  9.71 us (5%)
    all_gather x1, waiting for transfers between devices, gather_copy(): return lax.all_gather(halves, 'gz', axis=2, tiled=True)  78.3 us
    psum x4, blocking collectives, by_axis(): x = lax.psum(x, axis)  34.8 us
    all_to_all x4, starting transfers between devices, copy_for_each(): lax.all_to_all(jnp.broadcast_to(x[None], (length, *x.shape)), axis, 0, 0,...  20.4 us
    all_to_all x4, waiting for transfers between devices, copy_for_each(): lax.all_to_all(jnp.broadcast_to(x[None], (length, *x.shape)), axis, 0, 0,...  10.9 us
    unnamed x11, local copies, waits for them, and re-layouts  7.25 us
    convert_element_type x1, other arithmetic, body(): copy_half = new_params.astype(jnp.bfloat16)  6.17 us
  transfers between devices with their start and end apart: 5, of which 4 were waited for; matrix products, arithmetic and copies ran while one was open for 3% of the time, Pallas kernels for 0%

commit v1 on v0

v1 whole, which is shorter than its diff:
```python
import functools

import jax
import jax.numpy as jnp
from jax import lax
from jax.experimental import pallas as pl
from jax.experimental.pallas import tpu as pltpu
from jax.sharding import PartitionSpec as P

MESH = pl.DeviceIdType.MESH
F32 = jnp.float32
BF16 = jnp.bfloat16

decay_rate = 0.842
tiny_term = 1e-30
step_share = 0.01
clip_limit = 1.0

LAYERS = 3
ROWS = 896
COLS = 384
STEP = 64
TILES = STEP // 8
HALF = ROWS // 2


def lanes(shape):
    return lax.broadcasted_iota(jnp.int32, shape, len(shape) - 1)


def total(x):
    return jnp.sum(jnp.sum(x, axis=0, keepdims=True), axis=1, keepdims=True)


def lane_of(x, k):
    return jnp.sum(jnp.where(lanes(x.shape) == k, x, 0.0), axis=1, keepdims=True)


def pack_rows(lane_dense):
    sub = lax.broadcasted_iota(jnp.int32, (8, 128), 0)
    lane = lanes((8, 128))
    source = lax.broadcasted_iota(jnp.int32, (128, 128), 0)
    target = lanes((128, 128))
    packed = None
    for k in range(ROWS // 128):
        pick = (target == source // 8 + 16 * k).astype(F32)
        spread = [
            jnp.where(lane % 8 == sub, jnp.broadcast_to(lane_dense[l : l + 1, 128 * k : 128 * (k + 1)], (8, 128)), 0.0)
            for l in range(LAYERS)
        ]
        part = jnp.dot(
            jnp.concatenate(spread, axis=0), pick, preferred_element_type=F32, precision=lax.Precision.HIGHEST
        )
        packed = part if packed is None else packed + part
    return packed


def unpack_rows(packed):
    sub = lax.broadcasted_iota(jnp.int32, (8, 128), 0)
    lane = lanes((8, 128))
    source = lax.broadcasted_iota(jnp.int32, (128, 128), 0)
    target = lanes((128, 128))
    out = []
    for k in range(ROWS // 128):
        pick = (source == target // 8 + 16 * k).astype(F32)
        part = jnp.dot(packed, pick, preferred_element_type=F32, precision=lax.Precision.HIGHEST)
        out.append(
            [
                jnp.sum(jnp.where(lane % 8 == sub, part[8 * l : 8 * (l + 1)], 0.0), axis=0, keepdims=True)
                for l in range(LAYERS)
            ]
        )
    return out


def step_kernel(
    sizes,
    p_h, g_h, rs_h, cs_h,
    np_o, rn_o, cn_o, ap_o, cc_o,
    g_v, rs_v, cs_v, row_x, col_x, plane_x, stack_x, rrb,
    load_sem, row_s, row_r, col_s, col_r, plane_s, plane_r, stack_s, stack_r,
    right_s, right_r, left_s, left_r,
):
    nx, ny, nz = sizes
    gx, gy, gz = lax.axis_index("gx"), lax.axis_index("gy"), lax.axis_index("gz")
    right, left = lax.rem(gz + 1, nz), lax.rem(gz + nz - 1, nz)
    columns = COLS * nz
    rows_all = ROWS * ny

    loads = [pltpu.make_async_copy(g_h.at[l], g_v.at[l], load_sem.at[l]) for l in range(LAYERS)]
    loads += [
        pltpu.make_async_copy(rs_h, rs_v, load_sem.at[LAYERS]),
        pltpu.make_async_copy(cs_h, cs_v, load_sem.at[LAYERS + 1]),
    ]
    loads += [pltpu.make_async_copy(p_h.at[l], np_o.at[l], load_sem.at[LAYERS + 2 + l]) for l in range(LAYERS)]
    for load in loads:
        load.start()

    def plane_peer(i):
        return lax.rem(gy + i // nz, ny), lax.rem(gz + i % nz, nz)

    barrier = pltpu.get_barrier_semaphore()
    for i in range(1, ny * nz):
        y, z = plane_peer(i)
        pl.semaphore_signal(barrier, inc=1, device_id={"gx": gx, "gy": y, "gz": z}, device_id_type=MESH)
    for i in range(1, nx):
        x = lax.rem(gx + i, nx)
        pl.semaphore_signal(barrier, inc=1, device_id={"gx": x, "gy": gy, "gz": gz}, device_id_type=MESH)

    lane = lanes((8, 128))
    for l in range(LAYERS):
        loads[l].wait()

        def stats(i, carry, l=l):
            packed, col_acc = carry
            x = g_v[l, pl.ds(pl.multiple_of(i * STEP, STEP), STEP), :].astype(F32)
            sq = x * x
            row = jnp.sum(sq[:, 0:128] + sq[:, 128:256] + sq[:, 256:384], axis=1, keepdims=True)
            for k in range(TILES):
                packed = jnp.where(lane == i * TILES + k, row[8 * k : 8 * k + 8], packed)
                col_acc = col_acc + sq[8 * k : 8 * k + 8, :]
            return packed, col_acc

        packed, col_acc = lax.fori_loop(0, ROWS // STEP, stats, (jnp.zeros((8, 128), F32), jnp.zeros((8, COLS), F32)))
        row_x[gz, l] = packed
        col_x[gy, :, COLS * l : COLS * (l + 1)] = jnp.sum(col_acc, axis=0, keepdims=True)

    pl.semaphore_wait(barrier, ny * nz - 1 + nx - 1)
    exchange = []
    for i in range(1, nz):
        exchange.append(
            pltpu.make_async_remote_copy(
                row_x.at[gz], row_x.at[gz], row_s.at[i - 1], row_r.at[i - 1],
                device_id={"gx": gx, "gy": gy, "gz": lax.rem(gz + i, nz)}, device_id_type=MESH,
            )
        )
    for i in range(1, ny):
        exchange.append(
            pltpu.make_async_remote_copy(
                col_x.at[gy], col_x.at[gy], col_s.at[i - 1], col_r.at[i - 1],
                device_id={"gx": gx, "gy": lax.rem(gy + i, ny), "gz": gz}, device_id_type=MESH,
            )
        )
    for copy in exchange:
        copy.start()

    weight_sq = []
    for l in range(LAYERS):
        loads[LAYERS + 2 + l].wait()

        def weigh(i, acc, l=l):
            w = np_o[l, pl.ds(pl.multiple_of(i * STEP, STEP), STEP), :]
            sq = w * w
            for k in range(TILES):
                acc = acc + sq[8 * k : 8 * k + 8, :]
            return acc

        weight_sq.append(total(lax.fori_loop(0, ROWS // STEP, weigh, jnp.zeros((8, COLS), F32))))
    loads[LAYERS].wait()
    loads[LAYERS + 1].wait()
    row_old = pack_rows(rs_v[...])

    for copy in exchange:
        copy.wait_recv()
    row_new, row_inv, col_inv, update_sq, row_total = [], [], [], [], []
    for l in range(LAYERS):
        row_sum = row_x[0, l]
        for k in range(1, nz):
            row_sum = row_sum + row_x[k, l]
        new = decay_rate * row_old[8 * l : 8 * l + 8] + (1.0 - decay_rate) * (row_sum / columns + tiny_term)
        row_new.append(new)
        row_inv.append(lax.rsqrt(new))
        row_total.append(total(jnp.where(lane < ROWS // 8, new, 0.0)))
        col_sum = col_x[0, :, COLS * l : COLS * (l + 1)]
        for k in range(1, ny):
            col_sum = col_sum + col_x[k, :, COLS * l : COLS * (l + 1)]
        new = decay_rate * cs_v[l : l + 1, :] + (1.0 - decay_rate) * (col_sum / rows_all + tiny_term)
        cn_o[l : l + 1, :] = new
        col_inv.append(lax.rsqrt(new))

    for l in range(LAYERS):

        def updates(i, acc, l=l):
            rows = pl.ds(pl.multiple_of(i * STEP, STEP), STEP)
            x = g_v[l, rows, :].astype(F32)
            u = x * col_inv[l]
            sq = u * u
            y = sq[:, 0:128] + sq[:, 128:256] + sq[:, 256:384]
            for k in range(TILES):
                inv = jnp.sum(jnp.where(lane == i * TILES + k, row_inv[l], 0.0), axis=1, keepdims=True)
                inv = jnp.broadcast_to(inv, (8, 128))
                rrb[l, pl.ds(pl.multiple_of(i * STEP + 8 * k, 8), 8), :] = inv
                acc = acc + y[8 * k : 8 * k + 8] * (inv * inv)
            return acc

        update_sq.append(total(lax.fori_loop(0, ROWS // STEP, updates, jnp.zeros((8, 128), F32))))

    row1 = lanes((1, 128))
    payload = jnp.zeros((1, 128), F32)
    for l in range(LAYERS):
        payload = jnp.where(row1 == l, update_sq[l], payload)
        payload = jnp.where(row1 == LAYERS + l, weight_sq[l], payload)
        payload = jnp.where(row1 == 2 * LAYERS + l, row_total[l], payload)
    plane_x[gy * nz + gz] = payload
    plane = []
    for i in range(1, ny * nz):
        y, z = plane_peer(i)
        plane.append(
            pltpu.make_async_remote_copy(
                plane_x.at[gy * nz + gz], plane_x.at[gy * nz + gz], plane_s.at[i - 1], plane_r.at[i - 1],
                device_id={"gx": gx, "gy": y, "gz": z}, device_id_type=MESH,
            )
        )
    for copy in plane:
        copy.start()
    for copy in plane:
        copy.wait_recv()
    sums = plane_x[0]
    for i in range(1, ny * nz):
        sums = sums + plane_x[i]

    mean_row = [lane_of(sums, 2 * LAYERS + l) / (nz * rows_all) for l in range(LAYERS)]
    here = jnp.zeros((1, 1), F32)
    for l in range(LAYERS):
        here = here + mean_row[l] * lane_of(sums, l)
    stack_x[gx] = jnp.broadcast_to(here, (1, 128))
    stack = []
    for i in range(1, nx):
        stack.append(
            pltpu.make_async_remote_copy(
                stack_x.at[gx], stack_x.at[gx], stack_s.at[i - 1], stack_r.at[i - 1],
                device_id={"gx": lax.rem(gx + i, nx), "gy": gy, "gz": gz}, device_id_type=MESH,
            )
        )
    for copy in stack:
        copy.start()
    for copy in stack:
        copy.wait_recv()
    everything = stack_x[0]
    for i in range(1, nx):
        everything = everything + stack_x[i]
    entries = float(nx * LAYERS * rows_all * columns)
    clip = jnp.maximum(1.0, jnp.sqrt(everything / entries) / clip_limit)
    scale = []
    for l in range(LAYERS):
        weight = jnp.sqrt(lane_of(sums, LAYERS + l) / (rows_all * columns))
        scale.append(weight * jnp.sqrt(mean_row[l]) / clip)

    def apply(l, h):
        def some(i, carry):
            rows = pl.ds(pl.multiple_of(h * HALF + i * STEP, STEP), STEP)
            factor = rrb[l, rows, :] * scale[l]
            x = g_v[l, rows, :].astype(F32) * col_inv[l]
            w = np_o[l, rows, :]
            step = jnp.concatenate([x[:, 128 * k : 128 * k + 128] * factor for k in range(COLS // 128)], axis=1)
            new = w - step_share * step
            ap_o[l, rows, :] = step
            np_o[l, rows, :] = new
            cc_o[gz, l, rows, :] = new.astype(BF16)
            return carry

        lax.fori_loop(0, HALF // STEP, some, 0)

    def piece(owner, l, h):
        return cc_o.at[owner, l, pl.ds(h * HALF, HALF), :]

    def to_right(owner, l, h, n):
        return pltpu.make_async_remote_copy(
            piece(owner, l, h), piece(owner, l, h), right_s.at[n], right_r.at[n],
            device_id={"gx": gx, "gy": gy, "gz": right}, device_id_type=MESH,
        )

    def to_left(owner, l, h, n):
        return pltpu.make_async_remote_copy(
            piece(owner, l, h), piece(owner, l, h), left_s.at[n], left_r.at[n],
            device_id={"gx": gx, "gy": gy, "gz": left}, device_id_type=MESH,
        )

    rights, lefts = [], []
    for l in range(LAYERS):
        apply(l, 0)
        rights.append(to_right(gz, l, 0, l))
        rights[-1].start()
        apply(l, 1)
        lefts.append(to_left(gz, l, 1, l))
        lefts[-1].start()
    for l in range(LAYERS):
        rights.append(to_right(gz, l, 1, LAYERS + l))
        rights[-1].start()
        lefts.append(to_left(gz, l, 0, LAYERS + l))
        lefts[-1].start()

    new_rows = unpack_rows(jnp.concatenate(row_new, axis=0))
    for k in range(ROWS // 128):
        for l in range(LAYERS):
            rn_o[l : l + 1, 128 * k : 128 * (k + 1)] = new_rows[k][l]

    for l in range(LAYERS):
        rights[l].wait_recv()
        rights.append(to_right(left, l, 0, 2 * LAYERS + l))
        rights[-1].start()
        lefts[l].wait_recv()
        lefts.append(to_left(right, l, 1, 2 * LAYERS + l))
        lefts[-1].start()
    for n in range(LAYERS, 3 * LAYERS):
        rights[n].wait_recv()
        lefts[n].wait_recv()
    for copy in exchange + plane + stack + rights + lefts:
        copy.wait_send()


def write_kernel(np_v, rn_v, cn_v, ap_v, cc_v, np_h, rn_h, cn_h, ap_h, cc_h, sem):
    copies = []

    def put(source, target):
        copies.append(pltpu.make_async_copy(source, target, sem.at[len(copies)]))
        copies[-1].start()

    for l in range(LAYERS):
        for k in range(cc_v.shape[0]):
            put(cc_v.at[k, l], cc_h.at[l, :, pl.ds(COLS * k, COLS)])
        put(np_v.at[l], np_h.at[l])
        put(ap_v.at[l], ap_h.at[l])
    put(rn_v, rn_h)
    put(cn_v, cn_h)
    for copy in copies:
        copy.wait()


def solution(mesh):
    nx, ny, nz = (mesh.shape[a] for a in ("gx", "gy", "gz"))

    def body(params, grads, row_state, col_state):
        V = pltpu.VMEM
        sem = pltpu.SemaphoreType.DMA
        kept = pl.pallas_call(
            functools.partial(step_kernel, (nx, ny, nz)),
            out_shape=[
                V((LAYERS, ROWS, COLS), F32),
                V((LAYERS, ROWS), F32),
                V((LAYERS, COLS), F32),
                V((LAYERS, ROWS, COLS), F32),
                V((nz, LAYERS, ROWS, COLS), BF16),
            ],
            in_specs=[pl.BlockSpec(memory_space=pltpu.HBM)] * 4,
            out_specs=[pl.BlockSpec(memory_space=V)] * 5,
            scratch_shapes=[
                V((LAYERS, ROWS, COLS), BF16),
                V((LAYERS, ROWS), F32),
                V((LAYERS, COLS), F32),
                V((nz, LAYERS, 8, 128), F32),
                V((ny, 1, LAYERS * COLS), F32),
                V((ny * nz, 1, 128), F32),
                V((nx, 1, 128), F32),
                V((LAYERS, ROWS, 128), F32),
                sem((2 * LAYERS + 2,)),
                sem((nz - 1,)), sem((nz - 1,)),
                sem((ny - 1,)), sem((ny - 1,)),
                sem((ny * nz - 1,)), sem((ny * nz - 1,)),
                sem((nx - 1,)), sem((nx - 1,)),
                sem((3 * LAYERS,)), sem((3 * LAYERS,)),
                sem((3 * LAYERS,)), sem((3 * LAYERS,)),
            ],
            compiler_params=pltpu.CompilerParams(
                collective_id=0, has_side_effects=True, vmem_limit_bytes=16 * 2**20
            ),
        )(*[pltpu.with_memory_space_constraint(a, pltpu.HBM) for a in (params, grads, row_state, col_state)])
        return tuple(
            pl.pallas_call(
                write_kernel,
                out_shape=[
                    jax.ShapeDtypeStruct((LAYERS, ROWS, COLS), F32),
                    jax.ShapeDtypeStruct((LAYERS, ROWS), F32),
                    jax.ShapeDtypeStruct((LAYERS, COLS), F32),
                    jax.ShapeDtypeStruct((LAYERS, ROWS, COLS), F32),
                    jax.ShapeDtypeStruct((LAYERS, ROWS, nz * COLS), BF16),
                ],
                in_specs=[pl.BlockSpec(memory_space=V)] * 5,
                out_specs=[pl.BlockSpec(memory_space=pltpu.HBM)] * 5,
                scratch_shapes=[sem((LAYERS * (nz + 2) + 2,))],
                compiler_params=pltpu.CompilerParams(vmem_limit_bytes=2**20),
            )(*kept)
        )

    return jax.shard_map(
        body,
        mesh=mesh,
        in_specs=(P("gx", "gy", "gz"), P("gx", "gy", "gz"), P("gx", "gy"), P("gx", "gz")),
        out_specs=(
            P("gx", "gy", "gz"),
            P("gx", "gy"),
            P("gx", "gz"),
            P("gx", "gy", "gz"),
            P("gx", "gy", None),
        ),
        check_vma=False,
    )
```

time: 183 us -> 102 us (0.56)
  Pallas kernels: 0 us -> 100 us
  waiting for transfers between devices: 89.2 us -> 0 us
  blocking collectives: 34.8 us -> 0 us
  starting transfers between devices: 20.4 us -> 0 us
  between operations: 14.8 us -> 0.64 us
  other arithmetic: 13.8 us -> 0 us
  local copies, waits for them, and re-layouts: 9.71 us -> 0 us
    pallas_call x0 -> x2, Pallas kernels: none -> 100 us  [the longest x1 94.1 us: body(): pl.pallas_call(functools.partial(step_kernel, (nx, ny, nz)), out_shape=[V...]
    all_gather x1 -> x0, waiting for transfers between devices: 78.3 us -> none  [gather_copy(): return lax.all_gather(halves, 'gz', axis=2, tiled=True)]
    psum x4 -> x0, blocking collectives: 34.8 us -> none  [by_axis(): x = lax.psum(x, axis)]
    all_to_all x4 -> x0, starting transfers between devices: 20.4 us -> none  [copy_for_each(): lax.all_to_all(jnp.broadcast_to(x[None], (length, *x.shape)), axis, 0, 0,...]
    all_to_all x4 -> x0, waiting for transfers between devices: 10.9 us -> none  [copy_for_each(): lax.all_to_all(jnp.broadcast_to(x[None], (length, *x.shape)), axis, 0, 0,...]
    reduce_sum x8 -> x0, other arithmetic: 7.58 us -> none  [the longest x1 2.64 us: factor_stats(): weight_sq = jnp.sum(weights * weights, axis=(1, 2))]
    unnamed x11 -> x0, local copies, waits for them, and re-layouts: 7.25 us -> none
    convert_element_type x1 -> x0, other arithmetic: 6.17 us -> none  [body(): copy_half = new_params.astype(jnp.bfloat16)]
  transfers between devices with their start and end apart: 5 -> 0, of which waited for: 4 -> 0; matrix products, arithmetic and copies ran while one was open for 3% -> 0% of each run, Pallas kernels for 0% -> 0%
where the time goes in v1:
time: 102 us; the launch traced here: 101 us
  Pallas kernels  100 us (98%)
    pallas_call x1, Pallas kernels, body(): pl.pallas_call(functools.partial(step_kernel, (nx, ny, nz)), out_shape=[V...  94.1 us
    pallas_call x1, Pallas kernels, body(): pl.pallas_call(write_kernel, out_shape=[jax.ShapeDtypeStruct((LAYERS, ROW...  5.97 us

profile of v1, /device:TPU:1, one launch (start us, length us, event | category | flops | bytes accessed | tf_op | source)
XLA Modules:
  0.0 100.7 jit_solution(2358916131358358035)
XLA Ops:
  0.6 94.1 %shard_map.83 = (f32[3,896,384]{2,1,0:T(8,128)S(1)}, f32[3,896]{1,0:T(4,128)S(1)}, f32[3,384]{1,0:T(4,128)S(1)}, f32[3,896,384]{2,1,0:T(8,128)S(1)}, bf16[4,3,896,384]{3,2,1,0:T(8,128)(2,1)S(1)}) custom-call(f32[3,896,384]{2,1,0:T(8,128)} %p_h.1, bf16[3,896,384]{2,1,0:T(8,128)(2,1)} %g_h.1, f32[3,896]{1,0:T(4,128)} %rs_h.1, f32[3,384]{1,0:T(4,128)} %cs_h.1), custom_call_target="tpu_custom_call" | custom-call | tf_op jit(solution)/shard_map/pallas_call | solution.py:336
  94.7 6.0 %shard_map.84 = (f32[3,896,384]{2,1,0:T(8,128)}, f32[3,896]{1,0:T(4,128)}, f32[3,384]{1,0:T(4,128)}, f32[3,896,384]{2,1,0:T(8,128)}, bf16[3,896,1536]{2,1,0:T(8,128)(2,1)}) custom-call(f32[3,896,384]{2,1,0:T(8,128)S(1)} %get-tuple-element.10.np_v, f32[3,896]{1,0:T(4,128)S(1)} %get-tuple-element.11.rn_v, f32[3,384]{1,0:T(4,128)S(1)} %get-tuple-element.12.cn_v, ...), custom_call_target="tpu_custom_call" | custom-call | tf_op jit(solution)/shard_map/pallas_call | solution.py:369

commit v2 on v1

--- a/solution.py
+++ b/solution.py
@@ -77,8 +77,8 @@
     sizes,
     p_h, g_h, rs_h, cs_h,
     np_o, rn_o, cn_o, ap_o, cc_o,
-    g_v, rs_v, cs_v, row_x, col_x, plane_x, stack_x, rrb,
-    load_sem, row_s, row_r, col_s, col_r, plane_s, plane_r, stack_s, stack_r,
+    g_v, rs_v, cs_v, row_x, col_x, all_x, row_inv, col_inv, rrb,
+    load_sem, row_s, row_r, col_s, col_r, all_s, all_r,
     right_s, right_r, left_s, left_r,
 ):
     nx, ny, nz = sizes
@@ -96,161 +96,141 @@
     for load in loads:
         load.start()
 
-    def plane_peer(i):
-        return lax.rem(gy + i // nz, ny), lax.rem(gz + i % nz, nz)
-
+    xs = [lax.rem(gx + i, nx) for i in range(nx)]
+    ys = [lax.rem(gy + i, ny) for i in range(ny)]
+    zs = [lax.rem(gz + i, nz) for i in range(nz)]
     barrier = pltpu.get_barrier_semaphore()
-    for i in range(1, ny * nz):
-        y, z = plane_peer(i)
-        pl.semaphore_signal(barrier, inc=1, device_id={"gx": gx, "gy": y, "gz": z}, device_id_type=MESH)
-    for i in range(1, nx):
-        x = lax.rem(gx + i, nx)
-        pl.semaphore_signal(barrier, inc=1, device_id={"gx": x, "gy": gy, "gz": gz}, device_id_type=MESH)
+    met = [(i, j, 0) for i in range(nx) for j in range(ny) if i or j] + [(0, 0, k) for k in range(1, nz)]
+    for i, j, k in met:
+        pl.semaphore_signal(barrier, inc=1, device_id={"gx": xs[i], "gy": ys[j], "gz": zs[k]}, device_id_type=MESH)
 
     lane = lanes((8, 128))
-    for l in range(LAYERS):
-        loads[l].wait()
-
-        def stats(i, carry, l=l):
-            packed, col_acc = carry
-            x = g_v[l, pl.ds(pl.multiple_of(i * STEP, STEP), STEP), :].astype(F32)
+
+    def stats(l, carry):
+        pltpu.make_async_copy(g_h.at[l], g_v.at[l], load_sem.at[l]).wait()
+        packed = jnp.zeros((8, 128), F32)
+        col_acc = jnp.zeros((8, COLS), F32)
+        for t in range(ROWS // 16):
+            x = g_v[l, 16 * t : 16 * t + 16, :].astype(F32)
             sq = x * x
             row = jnp.sum(sq[:, 0:128] + sq[:, 128:256] + sq[:, 256:384], axis=1, keepdims=True)
-            for k in range(TILES):
-                packed = jnp.where(lane == i * TILES + k, row[8 * k : 8 * k + 8], packed)
-                col_acc = col_acc + sq[8 * k : 8 * k + 8, :]
-            return packed, col_acc
-
-        packed, col_acc = lax.fori_loop(0, ROWS // STEP, stats, (jnp.zeros((8, 128), F32), jnp.zeros((8, COLS), F32)))
+            packed = jnp.where(lane == 2 * t, row[0:8], packed)
+            packed = jnp.where(lane == 2 * t + 1, row[8:16], packed)
+            col_acc = col_acc + sq[0:8] + sq[8:16]
         row_x[gz, l] = packed
-        col_x[gy, :, COLS * l : COLS * (l + 1)] = jnp.sum(col_acc, axis=0, keepdims=True)
-
-    pl.semaphore_wait(barrier, ny * nz - 1 + nx - 1)
+        col_x[gy, l] = jnp.sum(col_acc, axis=0, keepdims=True)
+        return carry
+
+    lax.fori_loop(0, LAYERS, stats, 0)
+
+    pl.semaphore_wait(barrier, len(met))
     exchange = []
     for i in range(1, nz):
         exchange.append(
             pltpu.make_async_remote_copy(
                 row_x.at[gz], row_x.at[gz], row_s.at[i - 1], row_r.at[i - 1],
-                device_id={"gx": gx, "gy": gy, "gz": lax.rem(gz + i, nz)}, device_id_type=MESH,
+                device_id={"gx": gx, "gy": gy, "gz": zs[i]}, device_id_type=MESH,
             )
         )
     for i in range(1, ny):
         exchange.append(
             pltpu.make_async_remote_copy(
                 col_x.at[gy], col_x.at[gy], col_s.at[i - 1], col_r.at[i - 1],
-                device_id={"gx": gx, "gy": lax.rem(gy + i, ny), "gz": gz}, device_id_type=MESH,
+                device_id={"gx": gx, "gy": ys[i], "gz": gz}, device_id_type=MESH,
             )
         )
     for copy in exchange:
         copy.start()
 
-    weight_sq = []
-    for l in range(LAYERS):
-        loads[LAYERS + 2 + l].wait()
-
-        def weigh(i, acc, l=l):
+    row1 = lanes((1, 128))
+
+    def weigh(l, payload):
+        pltpu.make_async_copy(p_h.at[l], np_o.at[l], load_sem.at[LAYERS + 2 + l]).wait()
+
+        def some(i, acc):
             w = np_o[l, pl.ds(pl.multiple_of(i * STEP, STEP), STEP), :]
             sq = w * w
             for k in range(TILES):
                 acc = acc + sq[8 * k : 8 * k + 8, :]
             return acc
 
-        weight_sq.append(total(lax.fori_loop(0, ROWS // STEP, weigh, jnp.zeros((8, COLS), F32))))
+        squares = lax.fori_loop(0, ROWS // STEP, some, jnp.zeros((8, COLS), F32))
+        return jnp.where(row1 == LAYERS + l, total(squares), payload)
+
+    payload = lax.fori_loop(0, LAYERS, weigh, jnp.zeros((1, 128), F32))
     loads[LAYERS].wait()
     loads[LAYERS + 1].wait()
     row_old = pack_rows(rs_v[...])
 
     for copy in exchange:
         copy.wait_recv()
-    row_new, row_inv, col_inv, update_sq, row_total = [], [], [], [], []
+    row_new = []
     for l in range(LAYERS):
         row_sum = row_x[0, l]
         for k in range(1, nz):
             row_sum = row_sum + row_x[k, l]
         new = decay_rate * row_old[8 * l : 8 * l + 8] + (1.0 - decay_rate) * (row_sum / columns + tiny_term)
         row_new.append(new)
-        row_inv.append(lax.rsqrt(new))
-        row_total.append(total(jnp.where(lane < ROWS // 8, new, 0.0)))
-        col_sum = col_x[0, :, COLS * l : COLS * (l + 1)]
+        row_inv[l] = lax.rsqrt(new)
+        payload = jnp.where(row1 == 2 * LAYERS + l, total(jnp.where(lane < ROWS // 8, new, 0.0)), payload)
+        col_sum = col_x[0, l]
         for k in range(1, ny):
-            col_sum = col_sum + col_x[k, :, COLS * l : COLS * (l + 1)]
+            col_sum = col_sum + col_x[k, l]
         new = decay_rate * cs_v[l : l + 1, :] + (1.0 - decay_rate) * (col_sum / rows_all + tiny_term)
         cn_o[l : l + 1, :] = new
-        col_inv.append(lax.rsqrt(new))
-
-    for l in range(LAYERS):
-
-        def updates(i, acc, l=l):
-            rows = pl.ds(pl.multiple_of(i * STEP, STEP), STEP)
-            x = g_v[l, rows, :].astype(F32)
-            u = x * col_inv[l]
+        col_inv[l] = lax.rsqrt(new)
+
+    def updates(l, payload):
+        acc = jnp.zeros((8, 128), F32)
+        inv_packed = row_inv[l]
+        inv_col = col_inv[l]
+        for t in range(ROWS // 16):
+            x = g_v[l, 16 * t : 16 * t + 16, :].astype(F32)
+            u = x * inv_col
             sq = u * u
             y = sq[:, 0:128] + sq[:, 128:256] + sq[:, 256:384]
-            for k in range(TILES):
-                inv = jnp.sum(jnp.where(lane == i * TILES + k, row_inv[l], 0.0), axis=1, keepdims=True)
+            for k in range(2):
+                inv = jnp.sum(jnp.where(lane == 2 * t + k, inv_packed, 0.0), axis=1, keepdims=True)
                 inv = jnp.broadcast_to(inv, (8, 128))
-                rrb[l, pl.ds(pl.multiple_of(i * STEP + 8 * k, 8), 8), :] = inv
+                rrb[l, 16 * t + 8 * k : 16 * t + 8 * k + 8, :] = inv
                 acc = acc + y[8 * k : 8 * k + 8] * (inv * inv)
-            return acc
-
-        update_sq.append(total(lax.fori_loop(0, ROWS // STEP, updates, jnp.zeros((8, 128), F32))))
-
-    row1 = lanes((1, 128))
-    payload = jnp.zeros((1, 128), F32)
-    for l in range(LAYERS):
-        payload = jnp.where(row1 == l, update_sq[l], payload)
-        payload = jnp.where(row1 == LAYERS + l, weight_sq[l], payload)
-        payload = jnp.where(row1 == 2 * LAYERS + l, row_total[l], payload)
-    plane_x[gy * nz + gz] = payload
-    plane = []
-    for i in range(1, ny * nz):
-        y, z = plane_peer(i)
-        plane.append(
-            pltpu.make_async_remote_copy(
-                plane_x.at[gy * nz + gz], plane_x.at[gy * nz + gz], plane_s.at[i - 1], plane_r.at[i - 1],
-                device_id={"gx": gx, "gy": y, "gz": z}, device_id_type=MESH,
-            )
-        )
-    for copy in plane:
-        copy.start()
-    for copy in plane:
-        copy.wait_recv()
-    sums = plane_x[0]
-    for i in range(1, ny * nz):
-        sums = sums + plane_x[i]
-
-    mean_row = [lane_of(sums, 2 * LAYERS + l) / (nz * rows_all) for l in range(LAYERS)]
-    here = jnp.zeros((1, 1), F32)
-    for l in range(LAYERS):
-        here = here + mean_row[l] * lane_of(sums, l)
-    stack_x[gx] = jnp.broadcast_to(here, (1, 128))
-    stack = []
-    for i in range(1, nx):
-        stack.append(
-            pltpu.make_async_remote_copy(
-                stack_x.at[gx], stack_x.at[gx], stack_s.at[i - 1], stack_r.at[i - 1],
-                device_id={"gx": lax.rem(gx + i, nx), "gy": gy, "gz": gz}, device_id_type=MESH,
-            )
-        )
-    for copy in stack:
-        copy.start()
-    for copy in stack:
-        copy.wait_recv()
-    everything = stack_x[0]
-    for i in range(1, nx):
-        everything = everything + stack_x[i]
+        return jnp.where(row1 == l, total(acc), payload)
+
+    payload = lax.fori_loop(0, LAYERS, updates, payload)
+
+    all_x[(gx * ny + gy) * nz + gz] = payload
+    mine = all_x.at[(gx * ny + gy) * nz + gz]
+
+    def far(at):
+        return sum(min(a, n - a) for a, n in zip((at[0], at[1] // 2, at[2]), (nx, ny // 2, nz)))
+
+    others = [(i, j, k) for i in range(nx) for j in range(ny) for k in range(nz) if i or j or k]
+    for i, j, k in sorted(others, key=far, reverse=True):
+        pltpu.make_async_remote_copy(
+            mine, mine, all_s, all_r,
+            device_id={"gx": xs[i], "gy": ys[j], "gz": zs[k]}, device_id_type=MESH,
+        ).start()
+    pltpu.make_async_copy(all_x.at[pl.ds(0, len(others))], all_x.at[pl.ds(0, len(others))], all_r).wait()
+    everything = jnp.zeros((1, 1), F32)
+    scale = [jnp.zeros((1, 1), F32)] * LAYERS
+    for i in range(nx):
+        sums = jnp.sum(all_x[i * ny * nz : (i + 1) * ny * nz], axis=0)
+        for l in range(LAYERS):
+            mean_row = lane_of(sums, 2 * LAYERS + l) / (nz * rows_all)
+            everything = everything + mean_row * lane_of(sums, l)
+            root = jnp.sqrt(lane_of(sums, LAYERS + l) / (rows_all * columns)) * jnp.sqrt(mean_row)
+            scale[l] = jnp.where(gx == i, root, scale[l])
     entries = float(nx * LAYERS * rows_all * columns)
     clip = jnp.maximum(1.0, jnp.sqrt(everything / entries) / clip_limit)
-    scale = []
-    for l in range(LAYERS):
-        weight = jnp.sqrt(lane_of(sums, LAYERS + l) / (rows_all * columns))
-        scale.append(weight * jnp.sqrt(mean_row[l]) / clip)
+    scale = [one / clip for one in scale]
 
     def apply(l, h):
+        inv_col = col_inv[l]
+
         def some(i, carry):
             rows = pl.ds(pl.multiple_of(h * HALF + i * STEP, STEP), STEP)
             factor = rrb[l, rows, :] * scale[l]
-            x = g_v[l, rows, :].astype(F32) * col_inv[l]
+            x = g_v[l, rows, :].astype(F32) * inv_col
             w = np_o[l, rows, :]
             step = jnp.concatenate([x[:, 128 * k : 128 * k + 128] * factor for k in range(COLS // 128)], axis=1)
             new = w - step_share * step
@@ -305,8 +285,9 @@
     for n in range(LAYERS, 3 * LAYERS):
         rights[n].wait_recv()
         lefts[n].wait_recv()
-    for copy in exchange + plane + stack + rights + lefts:
+    for copy in exchange + rights + lefts:
         copy.wait_send()
+    pltpu.make_async_copy(all_x.at[pl.ds(0, len(others))], all_x.at[pl.ds(0, len(others))], all_s).wait()
 
 
 def write_kernel(np_v, rn_v, cn_v, ap_v, cc_v, np_h, rn_h, cn_h, ap_h, cc_h, sem):
@@ -349,15 +330,15 @@
                 V((LAYERS, ROWS), F32),
                 V((LAYERS, COLS), F32),
                 V((nz, LAYERS, 8, 128), F32),
-                V((ny, 1, LAYERS * COLS), F32),
-                V((ny * nz, 1, 128), F32),
-                V((nx, 1, 128), F32),
+                V((ny, LAYERS, 1, COLS), F32),
+                V((nx * ny * nz, 1, 128), F32),
+                V((LAYERS, 8, 128), F32),
+                V((LAYERS, 1, COLS), F32),
                 V((LAYERS, ROWS, 128), F32),
                 sem((2 * LAYERS + 2,)),
                 sem((nz - 1,)), sem((nz - 1,)),
                 sem((ny - 1,)), sem((ny - 1,)),
-                sem((ny * nz - 1,)), sem((ny * nz - 1,)),
-                sem((nx - 1,)), sem((nx - 1,)),
+                sem, sem,
                 sem((3 * LAYERS,)), sem((3 * LAYERS,)),
                 sem((3 * LAYERS,)), sem((3 * LAYERS,)),
             ],

time: 102 us -> 94.3 us (0.925); the launches traced: 101 us -> 94.2 us
  Pallas kernels: 100 us -> 93.6 us
    pallas_call x1, Pallas kernels: 94.1 us -> 87.6 us  [body(): pl.pallas_call(functools.partial(step_kernel, (nx, ny, nz)), out_shape=[V...]
where the time goes in v2:
time: 94.3 us; the launch traced here: 94.2 us
  Pallas kernels  93.6 us (99%)
    pallas_call x1, Pallas kernels, body(): pl.pallas_call(functools.partial(step_kernel, (nx, ny, nz)), out_shape=[V...  87.6 us
    pallas_call x1, Pallas kernels, body(): pl.pallas_call(write_kernel, out_shape=[jax.ShapeDtypeStruct((LAYERS, ROW...  5.97 us

profile of v2, /device:TPU:1, one launch (start us, length us, event | category | flops | bytes accessed | tf_op | source)
XLA Modules:
  0.0 94.2 jit_solution(1720449136949264129)
XLA Ops:
  0.6 87.6 %shard_map.83 = (f32[3,896,384]{2,1,0:T(8,128)S(1)}, f32[3,896]{1,0:T(4,128)S(1)}, f32[3,384]{1,0:T(4,128)S(1)}, f32[3,896,384]{2,1,0:T(8,128)S(1)}, bf16[4,3,896,384]{3,2,1,0:T(8,128)(2,1)S(1)}) custom-call(f32[3,896,384]{2,1,0:T(8,128)} %p_h.1, bf16[3,896,384]{2,1,0:T(8,128)(2,1)} %g_h.1, f32[3,896]{1,0:T(4,128)} %rs_h.1, f32[3,384]{1,0:T(4,128)} %cs_h.1), custom_call_target="tpu_custom_call" | custom-call | tf_op jit(solution)/shard_map/pallas_call | solution.py:317
  88.2 6.0 %shard_map.84 = (f32[3,896,384]{2,1,0:T(8,128)}, f32[3,896]{1,0:T(4,128)}, f32[3,384]{1,0:T(4,128)}, f32[3,896,384]{2,1,0:T(8,128)}, bf16[3,896,1536]{2,1,0:T(8,128)(2,1)}) custom-call(f32[3,896,384]{2,1,0:T(8,128)S(1)} %get-tuple-element.10.np_v, f32[3,896]{1,0:T(4,128)S(1)} %get-tuple-element.11.rn_v, f32[3,384]{1,0:T(4,128)S(1)} %get-tuple-element.12.cn_v, ...), custom_call_target="tpu_custom_call" | custom-call | tf_op jit(solution)/shard_map/pallas_call | solution.py:350

commit v3 on v2

--- a/solution.py
+++ b/solution.py
@@ -19,9 +19,15 @@
 LAYERS = 3
 ROWS = 896
 COLS = 384
-STEP = 64
+STEP = 32
 TILES = STEP // 8
-HALF = ROWS // 2
+PIECE = ROWS // 4
+PIECES = 2 * LAYERS
+EARLY = (0, 6)
+
+
+def place(kind, n):
+    return n // 2, (2 * kind + n % 2) * PIECE
 
 
 def lanes(shape):
@@ -224,11 +230,11 @@
     clip = jnp.maximum(1.0, jnp.sqrt(everything / entries) / clip_limit)
     scale = [one / clip for one in scale]
 
-    def apply(l, h):
+    def apply(l, first):
         inv_col = col_inv[l]
 
         def some(i, carry):
-            rows = pl.ds(pl.multiple_of(h * HALF + i * STEP, STEP), STEP)
+            rows = pl.ds(pl.multiple_of(first + i * STEP, STEP), STEP)
             factor = rrb[l, rows, :] * scale[l]
             x = g_v[l, rows, :].astype(F32) * inv_col
             w = np_o[l, rows, :]
@@ -239,73 +245,160 @@
             cc_o[gz, l, rows, :] = new.astype(BF16)
             return carry
 
-        lax.fori_loop(0, HALF // STEP, some, 0)
-
-    def piece(owner, l, h):
-        return cc_o.at[owner, l, pl.ds(h * HALF, HALF), :]
-
-    def to_right(owner, l, h, n):
+        lax.fori_loop(0, PIECE // STEP, some, 0)
+
+    def send(owner, kind, n, way, number):
+        l, first = place(kind, n)
+        piece = cc_o.at[owner, l, pl.ds(first, PIECE), :]
         return pltpu.make_async_remote_copy(
-            piece(owner, l, h), piece(owner, l, h), right_s.at[n], right_r.at[n],
-            device_id={"gx": gx, "gy": gy, "gz": right}, device_id_type=MESH,
-        )
-
-    def to_left(owner, l, h, n):
-        return pltpu.make_async_remote_copy(
-            piece(owner, l, h), piece(owner, l, h), left_s.at[n], left_r.at[n],
-            device_id={"gx": gx, "gy": gy, "gz": left}, device_id_type=MESH,
-        )
-
-    rights, lefts = [], []
-    for l in range(LAYERS):
-        apply(l, 0)
-        rights.append(to_right(gz, l, 0, l))
-        rights[-1].start()
-        apply(l, 1)
-        lefts.append(to_left(gz, l, 1, l))
-        lefts[-1].start()
-    for l in range(LAYERS):
-        rights.append(to_right(gz, l, 1, LAYERS + l))
-        rights[-1].start()
-        lefts.append(to_left(gz, l, 0, LAYERS + l))
-        lefts[-1].start()
-
+            piece, piece, (right_s, left_s)[way].at[number], (right_r, left_r)[way].at[number],
+            device_id={"gx": gx, "gy": gy, "gz": (right, left)[way]}, device_id_type=MESH,
+        )
+
+    core = lax.rem(gy, 2)
+    own = ([send(gz, 0, n, 0, n) for n in range(PIECES)], [send(gz, 1, n, 1, n) for n in range(PIECES)])
+    last = ([send(gz, 1, n, 0, PIECES + n) for n in range(PIECES)], [send(gz, 0, n, 1, PIECES + n) for n in range(PIECES)])
+    on = (
+        [send(left, 0, n, 0, 2 * PIECES + n) for n in range(PIECES)],
+        [send(right, 1, n, 1, 2 * PIECES + n) for n in range(PIECES)],
+    )
+    for n in range(PIECES):
+        for way in range(2):
+            apply(*place(way, n))
+            own[way][n].start()
+
+    def extra(do):
+        for n in range(min(EARLY)):
+            for way in range(2):
+                do(last[way][n])
+
+        @pl.when(core == (0 if EARLY[0] > EARLY[1] else 1))
+        def _():
+            for n in range(min(EARLY), max(EARLY)):
+                for way in range(2):
+                    do(last[way][n])
+
+    extra(lambda copy: copy.start())
     new_rows = unpack_rows(jnp.concatenate(row_new, axis=0))
     for k in range(ROWS // 128):
         for l in range(LAYERS):
             rn_o[l : l + 1, 128 * k : 128 * (k + 1)] = new_rows[k][l]
 
-    for l in range(LAYERS):
-        rights[l].wait_recv()
-        rights.append(to_right(left, l, 0, 2 * LAYERS + l))
-        rights[-1].start()
-        lefts[l].wait_recv()
-        lefts.append(to_left(right, l, 1, 2 * LAYERS + l))
-        lefts[-1].start()
-    for n in range(LAYERS, 3 * LAYERS):
-        rights[n].wait_recv()
-        lefts[n].wait_recv()
-    for copy in exchange + rights + lefts:
+    for n in range(PIECES):
+        for way in range(2):
+            own[way][n].wait_recv()
+            on[way][n].start()
+    for way in range(2):
+        for n in range(PIECES):
+            on[way][n].wait_recv()
+    extra(lambda copy: copy.wait_recv())
+    for copy in exchange + own[0] + own[1] + on[0] + on[1]:
         copy.wait_send()
+    extra(lambda copy: copy.wait_send())
     pltpu.make_async_copy(all_x.at[pl.ds(0, len(others))], all_x.at[pl.ds(0, len(others))], all_s).wait()
 
 
-def write_kernel(np_v, rn_v, cn_v, ap_v, cc_v, np_h, rn_h, cn_h, ap_h, cc_h, sem):
+def rest(core, early, late):
+    for n in range(PIECES):
+        for way in range(2):
+            if n < min(EARLY):
+                early(way, n)
+            elif n >= max(EARLY):
+                late(way, n)
+
+    ahead = 0 if EARLY[0] > EARLY[1] else 1
+    for mine, do in ((ahead, early), (1 - ahead, late)):
+
+        @pl.when(core == mine)
+        def _(do=do):
+            for n in range(min(EARLY), max(EARLY)):
+                for way in range(2):
+                    do(way, n)
+
+
+def columns_of(owner):
+    return pl.ds(pl.multiple_of(owner * COLS, COLS), COLS)
+
+
+def rest_kernel(nz, cc_v, after_h, late_o, right_s, right_r, left_s, left_r):
+    gx, gy, gz = lax.axis_index("gx"), lax.axis_index("gy"), lax.axis_index("gz")
+    right, left = lax.rem(gz + 1, nz), lax.rem(gz + nz - 1, nz)
+    barrier = pltpu.get_barrier_semaphore()
+    for z in (right, left):
+        pl.semaphore_signal(barrier, inc=1, device_id={"gx": gx, "gy": gy, "gz": z}, device_id_type=MESH)
+    pl.semaphore_wait(barrier, 2)
+
+    def send(way, n):
+        l, first = place(1 - way, n)
+        return pltpu.make_async_remote_copy(
+            cc_v.at[gz, l, pl.ds(first, PIECE), :], late_o.at[way, n],
+            (right_s, left_s)[way].at[n], (right_r, left_r)[way].at[n],
+            device_id={"gx": gx, "gy": gy, "gz": (right, left)[way]}, device_id_type=MESH,
+        )
+
+    def skip(way, n):
+        pass
+
+    core = lax.rem(gy, 2)
+    rest(core, skip, lambda way, n: send(way, n).start())
+    rest(core, skip, lambda way, n: send(way, n).wait())
+
+
+def write_kernel(nz, np_v, rn_v, cn_v, ap_v, cc_v, np_h, rn_h, cn_h, ap_h, cc_h, sem, part_sem):
+    gy, gz = lax.axis_index("gy"), lax.axis_index("gz")
+    right, left, across = lax.rem(gz + 1, nz), lax.rem(gz + nz - 1, nz), lax.rem(gz + 2, nz)
     copies = []
 
     def put(source, target):
         copies.append(pltpu.make_async_copy(source, target, sem.at[len(copies)]))
         copies[-1].start()
 
+    def part(way, n):
+        l, first = place(1 - way, n)
+        rows = pl.ds(first, PIECE)
+        owner = (left, right)[way]
+        return pltpu.make_async_copy(
+            cc_v.at[owner, l, rows, :], cc_h.at[l, rows, columns_of(owner)], part_sem.at[way * PIECES + n]
+        )
+
     for l in range(LAYERS):
-        for k in range(cc_v.shape[0]):
-            put(cc_v.at[k, l], cc_h.at[l, :, pl.ds(COLS * k, COLS)])
         put(np_v.at[l], np_h.at[l])
         put(ap_v.at[l], ap_h.at[l])
+        for owner in (gz, across):
+            put(cc_v.at[owner, l], cc_h.at[l, :, columns_of(owner)])
+        for kind, owner in ((0, left), (1, right)):
+            rows = pl.ds(2 * kind * PIECE, 2 * PIECE)
+            put(cc_v.at[owner, l, rows, :], cc_h.at[l, rows, columns_of(owner)])
     put(rn_v, rn_h)
     put(cn_v, cn_h)
+
+    def skip(way, n):
+        pass
+
+    core = lax.rem(gy, 2)
+    rest(core, lambda way, n: part(way, n).start(), skip)
     for copy in copies:
         copy.wait()
+    rest(core, lambda way, n: part(way, n).wait(), skip)
+
+
+def finish_kernel(nz, late_v, old_h, cc_h, part_sem):
+    gy, gz = lax.axis_index("gy"), lax.axis_index("gz")
+    right, left = lax.rem(gz + 1, nz), lax.rem(gz + nz - 1, nz)
+
+    def part(way, n):
+        l, first = place(1 - way, n)
+        rows = pl.ds(first, PIECE)
+        return pltpu.make_async_copy(
+            late_v.at[way, n], cc_h.at[l, rows, columns_of((left, right)[way])], part_sem.at[way * PIECES + n]
+        )
+
+    def skip(way, n):
+        pass
+
+    core = lax.rem(gy, 2)
+    rest(core, skip, lambda way, n: part(way, n).start())
+    rest(core, skip, lambda way, n: part(way, n).wait())
 
 
 def solution(mesh):
@@ -339,29 +432,45 @@
                 sem((nz - 1,)), sem((nz - 1,)),
                 sem((ny - 1,)), sem((ny - 1,)),
                 sem, sem,
-                sem((3 * LAYERS,)), sem((3 * LAYERS,)),
-                sem((3 * LAYERS,)), sem((3 * LAYERS,)),
+                sem((3 * PIECES,)), sem((3 * PIECES,)),
+                sem((3 * PIECES,)), sem((3 * PIECES,)),
             ],
             compiler_params=pltpu.CompilerParams(
                 collective_id=0, has_side_effects=True, vmem_limit_bytes=16 * 2**20
             ),
         )(*[pltpu.with_memory_space_constraint(a, pltpu.HBM) for a in (params, grads, row_state, col_state)])
-        return tuple(
-            pl.pallas_call(
-                write_kernel,
-                out_shape=[
-                    jax.ShapeDtypeStruct((LAYERS, ROWS, COLS), F32),
-                    jax.ShapeDtypeStruct((LAYERS, ROWS), F32),
-                    jax.ShapeDtypeStruct((LAYERS, COLS), F32),
-                    jax.ShapeDtypeStruct((LAYERS, ROWS, COLS), F32),
-                    jax.ShapeDtypeStruct((LAYERS, ROWS, nz * COLS), BF16),
-                ],
-                in_specs=[pl.BlockSpec(memory_space=V)] * 5,
-                out_specs=[pl.BlockSpec(memory_space=pltpu.HBM)] * 5,
-                scratch_shapes=[sem((LAYERS * (nz + 2) + 2,))],
-                compiler_params=pltpu.CompilerParams(vmem_limit_bytes=2**20),
-            )(*kept)
-        )
+        new_params, row_new, col_new, applied, compute = pl.pallas_call(
+            functools.partial(write_kernel, nz),
+            out_shape=[
+                jax.ShapeDtypeStruct((LAYERS, ROWS, COLS), F32),
+                jax.ShapeDtypeStruct((LAYERS, ROWS), F32),
+                jax.ShapeDtypeStruct((LAYERS, COLS), F32),
+                jax.ShapeDtypeStruct((LAYERS, ROWS, COLS), F32),
+                jax.ShapeDtypeStruct((LAYERS, ROWS, nz * COLS), BF16),
+            ],
+            in_specs=[pl.BlockSpec(memory_space=V)] * 5,
+            out_specs=[pl.BlockSpec(memory_space=pltpu.HBM)] * 5,
+            scratch_shapes=[sem((6 * LAYERS + 2,)), sem((2 * PIECES,))],
+            compiler_params=pltpu.CompilerParams(vmem_limit_bytes=2**20),
+        )(*kept)
+        late = pl.pallas_call(
+            functools.partial(rest_kernel, nz),
+            out_shape=V((2, PIECES, PIECE, COLS), BF16),
+            in_specs=[pl.BlockSpec(memory_space=V), pl.BlockSpec(memory_space=pltpu.HBM)],
+            out_specs=pl.BlockSpec(memory_space=V),
+            scratch_shapes=[sem((PIECES,)), sem((PIECES,)), sem((PIECES,)), sem((PIECES,))],
+            compiler_params=pltpu.CompilerParams(collective_id=1, has_side_effects=True, vmem_limit_bytes=2**20),
+        )(kept[4], pltpu.with_memory_space_constraint(col_new, pltpu.HBM))
+        compute = pl.pallas_call(
+            functools.partial(finish_kernel, nz),
+            out_shape=jax.ShapeDtypeStruct((LAYERS, ROWS, nz * COLS), BF16),
+            in_specs=[pl.BlockSpec(memory_space=V), pl.BlockSpec(memory_space=pltpu.HBM)],
+            out_specs=pl.BlockSpec(memory_space=pltpu.HBM),
+            scratch_shapes=[sem((2 * PIECES,))],
+            input_output_aliases={1: 0},
+            compiler_params=pltpu.CompilerParams(vmem_limit_bytes=2**20),
+        )(late, compute)
+        return new_params, row_new, col_new, applied, compute
 
     return jax.shard_map(
         body,

time: 94.3 us -> 90.2 us (0.957)
  the two profiles are of different devices: /device:TPU:1 before, /device:TPU:0 now
where the time goes in v3:
time: 90.2 us; the launch traced here: 90.1 us
  Pallas kernels  89.4 us (99%)
    pallas_call x1, Pallas kernels, body(): pl.pallas_call(functools.partial(step_kernel, (nx, ny, nz)), out_shape=[V...  66.5 us
    pallas_call x1, Pallas kernels, body(): pl.pallas_call(functools.partial(rest_kernel, nz), out_shape=V((2, PIECES...  16.1 us
    pallas_call x1, Pallas kernels, body(): pl.pallas_call(functools.partial(write_kernel, nz), out_shape=[jax.ShapeD...  5.39 us

profile of v3, /device:TPU:0, one launch (start us, length us, event | category | flops | bytes accessed | tf_op | source)
XLA Modules:
  0.0 90.1 jit_solution(347260299787073102)
XLA Ops:
  0.6 66.5 %shard_map.83 = (f32[3,896,384]{2,1,0:T(8,128)S(1)}, f32[3,896]{1,0:T(4,128)S(1)}, f32[3,384]{1,0:T(4,128)S(1)}, f32[3,896,384]{2,1,0:T(8,128)S(1)}, bf16[4,3,896,384]{3,2,1,0:T(8,128)(2,1)S(1)}) custom-call(f32[3,896,384]{2,1,0:T(8,128)} %p_h.1, bf16[3,896,384]{2,1,0:T(8,128)(2,1)} %g_h.1, f32[3,896]{1,0:T(4,128)} %rs_h.1, f32[3,384]{1,0:T(4,128)} %cs_h.1), custom_call_target="tpu_custom_call" | custom-call | tf_op jit(solution)/shard_map/pallas_call | solution.py:410
  67.1 5.4 %shard_map.84 = (f32[3,896,384]{2,1,0:T(8,128)}, f32[3,896]{1,0:T(4,128)}, f32[3,384]{1,0:T(4,128)}, f32[3,896,384]{2,1,0:T(8,128)}, bf16[3,896,1536]{2,1,0:T(8,128)(2,1)}) custom-call(f32[3,896,384]{2,1,0:T(8,128)S(1)} %get-tuple-element.15.np_v, f32[3,896]{1,0:T(4,128)S(1)} %get-tuple-element.16.rn_v, f32[3,384]{1,0:T(4,128)S(1)} %get-tuple-element.17.cn_v, ...), custom_call_target="tpu_custom_call" | custom-call | tf_op jit(solution)/shard_map/pallas_call | solution.py:442
  72.5 16.1 %shard_map.85.late_v = bf16[2,6,224,384]{3,2,1,0:T(8,128)(2,1)S(1)} custom-call(bf16[4,3,896,384]{3,2,1,0:T(8,128)(2,1)S(1)} %get-tuple-element.19.cc_v, f32[3,384]{1,0:T(4,128)} %get-tuple-element.12.after_h), custom_call_target="tpu_custom_call" | custom-call | tf_op jit(solution)/shard_map/pallas_call | solution.py:456
  88.7 1.4 %shard_map.86 = bf16[3,896,1536]{2,1,0:T(8,128)(2,1)} custom-call(bf16[2,6,224,384]{3,2,1,0:T(8,128)(2,1)S(1)} %shard_map.85.late_v, bf16[3,896,1536]{2,1,0:T(8,128)(2,1)} %get-tuple-element.24.old_h), custom_call_target="tpu_custom_call", output_to_operand_aliasing={{}: (1, {})} | custom-call | tf_op jit(solution)/shard_map/pallas_call | solution.py:464

commit v4 on v3

--- a/solution.py
+++ b/solution.py
@@ -19,19 +19,27 @@
 LAYERS = 3
 ROWS = 896
 COLS = 384
-STEP = 32
-TILES = STEP // 8
+STEP = 112
+RAW = 64
 PIECE = ROWS // 4
 PIECES = 2 * LAYERS
 EARLY = (0, 6)
 
 
 def place(kind, n):
-    return n // 2, (2 * kind + n % 2) * PIECE
+    first = (2 * kind + n % 2) * PIECE
+    cut = RAW if n == 0 else 0
+    return n // 2, first + cut, PIECE - cut
 
 
 def lanes(shape):
     return lax.broadcasted_iota(jnp.int32, shape, len(shape) - 1)
+
+
+def advance(weights, gradient, inv_col, factor):
+    scaled = gradient.astype(F32) * inv_col
+    step = jnp.concatenate([scaled[:, 128 * k : 128 * k + 128] * factor for k in range(COLS // 128)], axis=1)
+    return step, weights - step_share * step
 
 
 def total(x):
@@ -83,8 +91,9 @@
     sizes,
     p_h, g_h, rs_h, cs_h,
     np_o, rn_o, cn_o, ap_o, cc_o,
-    g_v, rs_v, cs_v, row_x, col_x, all_x, row_inv, col_inv, rrb,
-    load_sem, row_s, row_r, col_s, col_r, all_s, all_r,
+    g_v, rs_v, cs_v, raw_p, raw_g, inv_x, row_x, col_x, all_x, row_inv, col_inv, rrb,
+    told_line, told_plane, load_sem, row_s, row_r, col_s, col_r, all_s, all_r,
+    inv_s, inv_r, raw_right_s, raw_right_r, raw_left_s, raw_left_r,
     right_s, right_r, left_s, left_r,
 ):
     nx, ny, nz = sizes
@@ -106,9 +115,15 @@
     ys = [lax.rem(gy + i, ny) for i in range(ny)]
     zs = [lax.rem(gz + i, nz) for i in range(nz)]
     barrier = pltpu.get_barrier_semaphore()
-    met = [(i, j, 0) for i in range(nx) for j in range(ny) if i or j] + [(0, 0, k) for k in range(1, nz)]
-    for i, j, k in met:
-        pl.semaphore_signal(barrier, inc=1, device_id={"gx": xs[i], "gy": ys[j], "gz": zs[k]}, device_id_type=MESH)
+
+    def signal(sem, peers):
+        for i, j, k in peers:
+            pl.semaphore_signal(sem, inc=1, device_id={"gx": xs[i], "gy": ys[j], "gz": zs[k]}, device_id_type=MESH)
+
+    line_x = [(i, 0, 0) for i in range(1, nx)]
+    line_y = [(0, j, 0) for j in range(1, ny)]
+    line_z = [(0, 0, k) for k in range(1, nz)]
+    signal(barrier, line_x + line_y + line_z)
 
     lane = lanes((8, 128))
 
@@ -129,7 +144,9 @@
 
     lax.fori_loop(0, LAYERS, stats, 0)
 
-    pl.semaphore_wait(barrier, len(met))
+    pl.semaphore_wait(barrier, len(line_x + line_y + line_z))
+    for load in loads[LAYERS + 2 :]:
+        load.wait()
     exchange = []
     for i in range(1, nz):
         exchange.append(
@@ -147,23 +164,42 @@
         )
     for copy in exchange:
         copy.start()
+    signal(told_line, line_z)
+
+    def raw(way, number):
+        kind = way if number != 1 else 1 - way
+        owner = (left, right)[way] if number == 2 else gz
+        rows = pl.ds(2 * kind * PIECE, RAW)
+        sources = (raw_p.at[owner, kind], raw_g.at[owner, kind]) if number == 2 else (np_o.at[0, rows], g_v.at[0, rows])
+        return [
+            pltpu.make_async_remote_copy(
+                source, target.at[owner, kind],
+                (raw_right_s, raw_left_s)[way].at[2 * number + k], (raw_right_r, raw_left_r)[way].at[2 * number + k],
+                device_id={"gx": gx, "gy": gy, "gz": (right, left)[way]}, device_id_type=MESH,
+            )
+            for k, (source, target) in enumerate(zip(sources, (raw_p, raw_g)))
+        ]
+
+    raws = [[raw(way, number) for way in range(2)] for number in range(3)]
+    for pair in raws[0]:
+        for copy in pair:
+            copy.start()
 
     row1 = lanes((1, 128))
 
     def weigh(l, payload):
-        pltpu.make_async_copy(p_h.at[l], np_o.at[l], load_sem.at[LAYERS + 2 + l]).wait()
-
         def some(i, acc):
-            w = np_o[l, pl.ds(pl.multiple_of(i * STEP, STEP), STEP), :]
-            sq = w * w
-            for k in range(TILES):
-                acc = acc + sq[8 * k : 8 * k + 8, :]
+            for t in range(STEP // 8):
+                w = np_o[l, pl.ds(pl.multiple_of(i * STEP + 8 * t, 8), 8), :]
+                acc = acc + w * w
             return acc
 
         squares = lax.fori_loop(0, ROWS // STEP, some, jnp.zeros((8, COLS), F32))
         return jnp.where(row1 == LAYERS + l, total(squares), payload)
 
     payload = lax.fori_loop(0, LAYERS, weigh, jnp.zeros((1, 128), F32))
+    pl.semaphore_wait(told_line, len(line_z))
+    signal(told_plane, line_y)
     loads[LAYERS].wait()
     loads[LAYERS + 1].wait()
     row_old = pack_rows(rs_v[...])
@@ -185,6 +221,16 @@
         new = decay_rate * cs_v[l : l + 1, :] + (1.0 - decay_rate) * (col_sum / rows_all + tiny_term)
         cn_o[l : l + 1, :] = new
         col_inv[l] = lax.rsqrt(new)
+    inv_x[gz] = col_inv[0]
+    inverse = [
+        pltpu.make_async_remote_copy(
+            inv_x.at[gz], inv_x.at[gz], inv_s.at[i - 1], inv_r.at[i - 1],
+            device_id={"gx": gx, "gy": gy, "gz": zs[i]}, device_id_type=MESH,
+        )
+        for i in range(1, nz)
+    ]
+    for copy in inverse:
+        copy.start()
 
     def updates(l, payload):
         acc = jnp.zeros((8, 128), F32)
@@ -204,6 +250,7 @@
 
     payload = lax.fori_loop(0, LAYERS, updates, payload)
 
+    pl.semaphore_wait(told_plane, len(line_y))
     all_x[(gx * ny + gy) * nz + gz] = payload
     mine = all_x.at[(gx * ny + gy) * nz + gz]
 
@@ -216,6 +263,14 @@
             mine, mine, all_s, all_r,
             device_id={"gx": xs[i], "gy": ys[j], "gz": zs[k]}, device_id_type=MESH,
         ).start()
+    for pair in raws[1]:
+        for copy in pair:
+            copy.start()
+    for way in range(2):
+        for copy in raws[0][way]:
+            copy.wait_recv()
+        for copy in raws[2][way]:
+            copy.start()
     pltpu.make_async_copy(all_x.at[pl.ds(0, len(others))], all_x.at[pl.ds(0, len(others))], all_r).wait()
     everything = jnp.zeros((1, 1), F32)
     scale = [jnp.zeros((1, 1), F32)] * LAYERS
@@ -230,26 +285,37 @@
     clip = jnp.maximum(1.0, jnp.sqrt(everything / entries) / clip_limit)
     scale = [one / clip for one in scale]
 
-    def apply(l, first):
+    def apply(l, first, size):
         inv_col = col_inv[l]
 
+        tiles = size // 16
+        at_once = max(k for k in range(1, 12) if tiles % k == 0)
+
         def some(i, carry):
-            rows = pl.ds(pl.multiple_of(first + i * STEP, STEP), STEP)
-            factor = rrb[l, rows, :] * scale[l]
-            x = g_v[l, rows, :].astype(F32) * inv_col
-            w = np_o[l, rows, :]
-            step = jnp.concatenate([x[:, 128 * k : 128 * k + 128] * factor for k in range(COLS // 128)], axis=1)
-            new = w - step_share * step
-            ap_o[l, rows, :] = step
-            np_o[l, rows, :] = new
-            cc_o[gz, l, rows, :] = new.astype(BF16)
+            for t in range(at_once):
+                rows = pl.ds(pl.multiple_of(first + (i * at_once + t) * 16, 16), 16)
+                step, new = advance(np_o[l, rows, :], g_v[l, rows, :], inv_col, rrb[l, rows, :] * scale[l])
+                ap_o[l, rows, :] = step
+                np_o[l, rows, :] = new
+                cc_o[gz, l, rows, :] = new.astype(BF16)
             return carry
 
-        lax.fori_loop(0, PIECE // STEP, some, 0)
+        lax.fori_loop(0, tiles // at_once, some, 0)
+
+    def apply_raw(owner):
+        inv_col = inv_x[owner]
+        for kind in range(2):
+            for t in range(RAW // 16):
+                rows = pl.ds(2 * kind * PIECE + 16 * t, 16)
+                some = pl.ds(16 * t, 16)
+                _, new = advance(
+                    raw_p[owner, kind, some, :], raw_g[owner, kind, some, :], inv_col, rrb[0, rows, :] * scale[0]
+                )
+                cc_o[owner, 0, rows, :] = new.astype(BF16)
 
     def send(owner, kind, n, way, number):
-        l, first = place(kind, n)
-        piece = cc_o.at[owner, l, pl.ds(first, PIECE), :]
+        l, first, size = place(kind, n)
+        piece = cc_o.at[owner, l, pl.ds(first, size), :]
         return pltpu.make_async_remote_copy(
             piece, piece, (right_s, left_s)[way].at[number], (right_r, left_r)[way].at[number],
             device_id={"gx": gx, "gy": gy, "gz": (right, left)[way]}, device_id_type=MESH,
@@ -284,6 +350,20 @@
         for l in range(LAYERS):
             rn_o[l : l + 1, 128 * k : 128 * (k + 1)] = new_rows[k][l]
 
+    for copy in inverse:
+        copy.wait_recv()
+    for number in (1, 2):
+        for pair in raws[number]:
+            for copy in pair:
+                copy.wait_recv()
+    for i in range(1, nz):
+        apply_raw(zs[i])
+    for number in range(3):
+        for pair in raws[number]:
+            for copy in pair:
+                copy.wait_send()
+    for kind in range(2):
+        apply(0, 2 * kind * PIECE, RAW)
     for n in range(PIECES):
         for way in range(2):
             own[way][n].wait_recv()
@@ -292,7 +372,7 @@
         for n in range(PIECES):
             on[way][n].wait_recv()
     extra(lambda copy: copy.wait_recv())
-    for copy in exchange + own[0] + own[1] + on[0] + on[1]:
+    for copy in exchange + inverse + own[0] + own[1] + on[0] + on[1]:
         copy.wait_send()
     extra(lambda copy: copy.wait_send())
     pltpu.make_async_copy(all_x.at[pl.ds(0, len(others))], all_x.at[pl.ds(0, len(others))], all_s).wait()
@@ -329,9 +409,9 @@
     pl.semaphore_wait(barrier, 2)
 
     def send(way, n):
-        l, first = place(1 - way, n)
+        l, first, size = place(1 - way, n)
         return pltpu.make_async_remote_copy(
-            cc_v.at[gz, l, pl.ds(first, PIECE), :], late_o.at[way, n],
+            cc_v.at[gz, l, pl.ds(first, size), :], late_o.at[way, n, pl.ds(0, size), :],
             (right_s, left_s)[way].at[n], (right_r, left_r)[way].at[n],
             device_id={"gx": gx, "gy": gy, "gz": (right, left)[way]}, device_id_type=MESH,
         )
@@ -354,8 +434,8 @@
         copies[-1].start()
 
     def part(way, n):
-        l, first = place(1 - way, n)
-        rows = pl.ds(first, PIECE)
+        l, first, size = place(1 - way, n)
+        rows = pl.ds(first, size)
         owner = (left, right)[way]
         return pltpu.make_async_copy(
             cc_v.at[owner, l, rows, :], cc_h.at[l, rows, columns_of(owner)], part_sem.at[way * PIECES + n]
@@ -369,6 +449,9 @@
         for kind, owner in ((0, left), (1, right)):
             rows = pl.ds(2 * kind * PIECE, 2 * PIECE)
             put(cc_v.at[owner, l, rows, :], cc_h.at[l, rows, columns_of(owner)])
+    for kind, owner in ((1, left), (0, right)):
+        rows = pl.ds(2 * kind * PIECE, RAW)
+        put(cc_v.at[owner, 0, rows, :], cc_h.at[0, rows, columns_of(owner)])
     put(rn_v, rn_h)
     put(cn_v, cn_h)
 
@@ -387,10 +470,10 @@
     right, left = lax.rem(gz + 1, nz), lax.rem(gz + nz - 1, nz)
 
     def part(way, n):
-        l, first = place(1 - way, n)
-        rows = pl.ds(first, PIECE)
+        l, first, size = place(1 - way, n)
+        rows = pl.ds(first, size)
         return pltpu.make_async_copy(
-            late_v.at[way, n], cc_h.at[l, rows, columns_of((left, right)[way])], part_sem.at[way * PIECES + n]
+            late_v.at[way, n, pl.ds(0, size), :], cc_h.at[l, rows, columns_of((left, right)[way])], part_sem.at[way * PIECES + n]
         )
 
     def skip(way, n):
@@ -422,16 +505,22 @@
                 V((LAYERS, ROWS, COLS), BF16),
                 V((LAYERS, ROWS), F32),
                 V((LAYERS, COLS), F32),
+                V((nz, 2, RAW, COLS), F32),
+                V((nz, 2, RAW, COLS), BF16),
+                V((nz, 1, COLS), F32),
                 V((nz, LAYERS, 8, 128), F32),
                 V((ny, LAYERS, 1, COLS), F32),
                 V((nx * ny * nz, 1, 128), F32),
                 V((LAYERS, 8, 128), F32),
                 V((LAYERS, 1, COLS), F32),
                 V((LAYERS, ROWS, 128), F32),
+                pltpu.SemaphoreType.REGULAR, pltpu.SemaphoreType.REGULAR,
                 sem((2 * LAYERS + 2,)),
                 sem((nz - 1,)), sem((nz - 1,)),
                 sem((ny - 1,)), sem((ny - 1,)),
                 sem, sem,
+                sem((nz - 1,)), sem((nz - 1,)),
+                sem((6,)), sem((6,)), sem((6,)), sem((6,)),
                 sem((3 * PIECES,)), sem((3 * PIECES,)),
                 sem((3 * PIECES,)), sem((3 * PIECES,)),
             ],
@@ -450,7 +539,7 @@
             ],
             in_specs=[pl.BlockSpec(memory_space=V)] * 5,
             out_specs=[pl.BlockSpec(memory_space=pltpu.HBM)] * 5,
-            scratch_shapes=[sem((6 * LAYERS + 2,)), sem((2 * PIECES,))],
+            scratch_shapes=[sem((6 * LAYERS + 4,)), sem((2 * PIECES,))],
             compiler_params=pltpu.CompilerParams(vmem_limit_bytes=2**20),
         )(*kept)
         late = pl.pallas_call(

time: 90.2 us -> 88.5 us (0.981)
  Pallas kernels: 89.4 us -> 87.8 us
    pallas_call x1, Pallas kernels: 66.5 us -> 65.4 us  [body(): pl.pallas_call(functools.partial(step_kernel, (nx, ny, nz)), out_shape=[V...]
where the time goes in v4:
time: 88.5 us; the launch traced here: 88.4 us
  Pallas kernels  87.8 us (99%)
    pallas_call x1, Pallas kernels, body(): pl.pallas_call(functools.partial(step_kernel, (nx, ny, nz)), out_shape=[V...  65.4 us
    pallas_call x1, Pallas kernels, body(): pl.pallas_call(functools.partial(rest_kernel, nz), out_shape=V((2, PIECES...  15.6 us
    pallas_call x1, Pallas kernels, body(): pl.pallas_call(functools.partial(write_kernel, nz), out_shape=[jax.ShapeD...  5.42 us

profile of v4, /device:TPU:0, one launch (start us, length us, event | category | flops | bytes accessed | tf_op | source)
XLA Modules:
  0.0 88.4 jit_solution(8314459947041822750)
XLA Ops:
  0.6 65.4 %shard_map.83 = (f32[3,896,384]{2,1,0:T(8,128)S(1)}, f32[3,896]{1,0:T(4,128)S(1)}, f32[3,384]{1,0:T(4,128)S(1)}, f32[3,896,384]{2,1,0:T(8,128)S(1)}, bf16[4,3,896,384]{3,2,1,0:T(8,128)(2,1)S(1)}) custom-call(f32[3,896,384]{2,1,0:T(8,128)} %p_h.1, bf16[3,896,384]{2,1,0:T(8,128)(2,1)} %g_h.1, f32[3,896]{1,0:T(4,128)} %rs_h.1, f32[3,384]{1,0:T(4,128)} %cs_h.1), custom_call_target="tpu_custom_call" | custom-call | tf_op jit(solution)/shard_map/pallas_call | solution.py:493
  66.0 5.4 %shard_map.84 = (f32[3,896,384]{2,1,0:T(8,128)}, f32[3,896]{1,0:T(4,128)}, f32[3,384]{1,0:T(4,128)}, f32[3,896,384]{2,1,0:T(8,128)}, bf16[3,896,1536]{2,1,0:T(8,128)(2,1)}) custom-call(f32[3,896,384]{2,1,0:T(8,128)S(1)} %get-tuple-element.15.np_v, f32[3,896]{1,0:T(4,128)S(1)} %get-tuple-element.16.rn_v, f32[3,384]{1,0:T(4,128)S(1)} %get-tuple-element.17.cn_v, ...), custom_call_target="tpu_custom_call" | custom-call | tf_op jit(solution)/shard_map/pallas_call | solution.py:531
  71.4 15.6 %shard_map.85.late_v = bf16[2,6,224,384]{3,2,1,0:T(8,128)(2,1)S(1)} custom-call(bf16[4,3,896,384]{3,2,1,0:T(8,128)(2,1)S(1)} %get-tuple-element.19.cc_v, f32[3,384]{1,0:T(4,128)} %get-tuple-element.12.after_h), custom_call_target="tpu_custom_call" | custom-call | tf_op jit(solution)/shard_map/pallas_call | solution.py:545
  87.0 1.4 %shard_map.86 = bf16[3,896,1536]{2,1,0:T(8,128)(2,1)} custom-call(bf16[2,6,224,384]{3,2,1,0:T(8,128)(2,1)S(1)} %shard_map.85.late_v, bf16[3,896,1536]{2,1,0:T(8,128)(2,1)} %get-tuple-element.24.old_h), custom_call_target="tpu_custom_call", output_to_operand_aliasing={{}: (1, {})} | custom-call | tf_op jit(solution)/shard_map/pallas_call | solution.py:553

commit v5 on v4

--- a/solution.py
+++ b/solution.py
@@ -23,13 +23,20 @@
 RAW = 64
 PIECE = ROWS // 4
 PIECES = 2 * LAYERS
-EARLY = (0, 6)
+REST = 2
+LATE_CORE = 0
 
 
 def place(kind, n):
     first = (2 * kind + n % 2) * PIECE
     cut = RAW if n == 0 else 0
     return n // 2, first + cut, PIECE - cut
+
+
+def stay(kind, n):
+    cut = RAW if n == 0 else 0
+    layers = pl.ds(0, 1) if n == 0 else pl.ds(1, LAYERS - 1)
+    return layers, 2 * kind * PIECE + cut, 2 * PIECE - cut
 
 
 def lanes(shape):
@@ -91,7 +98,7 @@
     sizes,
     p_h, g_h, rs_h, cs_h,
     np_o, rn_o, cn_o, ap_o, cc_o,
-    g_v, rs_v, cs_v, raw_p, raw_g, inv_x, row_x, col_x, all_x, row_inv, col_inv, rrb,
+    g_v, rs_v, cs_v, raw_p, raw_g, inv_x, row_x, col_x, all_x, row_inv, col_inv, col_w, rrb,
     told_line, told_plane, load_sem, row_s, row_r, col_s, col_r, all_s, all_r,
     inv_s, inv_r, raw_right_s, raw_right_r, raw_left_s, raw_left_r,
     right_s, right_r, left_s, left_r,
@@ -192,6 +199,10 @@
             for t in range(STEP // 8):
                 w = np_o[l, pl.ds(pl.multiple_of(i * STEP + 8 * t, 8), 8), :]
                 acc = acc + w * w
+            for t in range(STEP // 16):
+                rows = pl.ds(pl.multiple_of(i * STEP + 16 * t, 16), 16)
+                x = g_v[l, rows, :].astype(F32)
+                ap_o[l, rows, :] = x * x
             return acc
 
         squares = lax.fori_loop(0, ROWS // STEP, some, jnp.zeros((8, COLS), F32))
@@ -204,7 +215,7 @@
     loads[LAYERS + 1].wait()
     row_old = pack_rows(rs_v[...])
 
-    for copy in exchange:
+    for copy in exchange[: nz - 1]:
         copy.wait_recv()
     row_new = []
     for l in range(LAYERS):
@@ -215,12 +226,32 @@
         row_new.append(new)
         row_inv[l] = lax.rsqrt(new)
         payload = jnp.where(row1 == 2 * LAYERS + l, total(jnp.where(lane < ROWS // 8, new, 0.0)), payload)
+
+    def updates(l, carry):
+        acc = [jnp.zeros((8, 128), F32)] * (COLS // 128)
+        inv_packed = row_inv[l]
+        for t in range(ROWS // 8):
+            inv = jnp.sum(jnp.where(lane == t, inv_packed, 0.0), axis=1, keepdims=True)
+            inv = jnp.broadcast_to(inv, (8, 128))
+            rrb[l, 8 * t : 8 * t + 8, :] = inv
+            inv = inv * inv
+            for k in range(COLS // 128):
+                acc[k] = acc[k] + ap_o[l, 8 * t : 8 * t + 8, 128 * k : 128 * k + 128] * inv
+        col_w[l] = jnp.sum(jnp.concatenate(acc, axis=1), axis=0, keepdims=True)
+        return carry
+
+    lax.fori_loop(0, LAYERS, updates, 0)
+    for copy in exchange[nz - 1 :]:
+        copy.wait_recv()
+    for l in range(LAYERS):
         col_sum = col_x[0, l]
         for k in range(1, ny):
             col_sum = col_sum + col_x[k, l]
         new = decay_rate * cs_v[l : l + 1, :] + (1.0 - decay_rate) * (col_sum / rows_all + tiny_term)
         cn_o[l : l + 1, :] = new
-        col_inv[l] = lax.rsqrt(new)
+        inv = lax.rsqrt(new)
+        col_inv[l] = inv
+        payload = jnp.where(row1 == l, total(col_w[l] * (inv * inv)), payload)
     inv_x[gz] = col_inv[0]
     inverse = [
         pltpu.make_async_remote_copy(
@@ -229,26 +260,6 @@
         )
         for i in range(1, nz)
     ]
-    for copy in inverse:
-        copy.start()
-
-    def updates(l, payload):
-        acc = jnp.zeros((8, 128), F32)
-        inv_packed = row_inv[l]
-        inv_col = col_inv[l]
-        for t in range(ROWS // 16):
-            x = g_v[l, 16 * t : 16 * t + 16, :].astype(F32)
-            u = x * inv_col
-            sq = u * u
-            y = sq[:, 0:128] + sq[:, 128:256] + sq[:, 256:384]
-            for k in range(2):
-                inv = jnp.sum(jnp.where(lane == 2 * t + k, inv_packed, 0.0), axis=1, keepdims=True)
-                inv = jnp.broadcast_to(inv, (8, 128))
-                rrb[l, 16 * t + 8 * k : 16 * t + 8 * k + 8, :] = inv
-                acc = acc + y[8 * k : 8 * k + 8] * (inv * inv)
-        return jnp.where(row1 == l, total(acc), payload)
-
-    payload = lax.fori_loop(0, LAYERS, updates, payload)
 
     pl.semaphore_wait(told_plane, len(line_y))
     all_x[(gx * ny + gy) * nz + gz] = payload
@@ -263,6 +274,8 @@
             mine, mine, all_s, all_r,
             device_id={"gx": xs[i], "gy": ys[j], "gz": zs[k]}, device_id_type=MESH,
         ).start()
+    for copy in inverse:
+        copy.start()
     for pair in raws[1]:
         for copy in pair:
             copy.start()
@@ -323,28 +336,26 @@
 
     core = lax.rem(gy, 2)
     own = ([send(gz, 0, n, 0, n) for n in range(PIECES)], [send(gz, 1, n, 1, n) for n in range(PIECES)])
-    last = ([send(gz, 1, n, 0, PIECES + n) for n in range(PIECES)], [send(gz, 0, n, 1, PIECES + n) for n in range(PIECES)])
+    last = []
+    for way in range(2):
+        for n in range(REST):
+            layers, first, size = stay(1 - way, n)
+            piece = cc_o.at[gz, layers, pl.ds(first, size), :]
+            last.append(
+                pltpu.make_async_remote_copy(
+                    piece, piece, (right_s, left_s)[way].at[2 * PIECES + n], (right_r, left_r)[way].at[2 * PIECES + n],
+                    device_id={"gx": gx, "gy": gy, "gz": (right, left)[way]}, device_id_type=MESH,
+                )
+            )
     on = (
-        [send(left, 0, n, 0, 2 * PIECES + n) for n in range(PIECES)],
-        [send(right, 1, n, 1, 2 * PIECES + n) for n in range(PIECES)],
+        [send(left, 0, n, 0, PIECES + n) for n in range(PIECES)],
+        [send(right, 1, n, 1, PIECES + n) for n in range(PIECES)],
     )
     for n in range(PIECES):
         for way in range(2):
             apply(*place(way, n))
             own[way][n].start()
 
-    def extra(do):
-        for n in range(min(EARLY)):
-            for way in range(2):
-                do(last[way][n])
-
-        @pl.when(core == (0 if EARLY[0] > EARLY[1] else 1))
-        def _():
-            for n in range(min(EARLY), max(EARLY)):
-                for way in range(2):
-                    do(last[way][n])
-
-    extra(lambda copy: copy.start())
     new_rows = unpack_rows(jnp.concatenate(row_new, axis=0))
     for k in range(ROWS // 128):
         for l in range(LAYERS):
@@ -368,32 +379,30 @@
         for way in range(2):
             own[way][n].wait_recv()
             on[way][n].start()
+
+    @pl.when(core != LATE_CORE)
+    def _():
+        for copy in last:
+            copy.start()
+
     for way in range(2):
         for n in range(PIECES):
             on[way][n].wait_recv()
-    extra(lambda copy: copy.wait_recv())
+
+    @pl.when(core != LATE_CORE)
+    def _():
+        for copy in last:
+            copy.wait()
+
     for copy in exchange + inverse + own[0] + own[1] + on[0] + on[1]:
         copy.wait_send()
-    extra(lambda copy: copy.wait_send())
     pltpu.make_async_copy(all_x.at[pl.ds(0, len(others))], all_x.at[pl.ds(0, len(others))], all_s).wait()
 
 
-def rest(core, early, late):
-    for n in range(PIECES):
-        for way in range(2):
-            if n < min(EARLY):
-                early(way, n)
-            elif n >= max(EARLY):
-                late(way, n)
-
-    ahead = 0 if EARLY[0] > EARLY[1] else 1
-    for mine, do in ((ahead, early), (1 - ahead, late)):
-
-        @pl.when(core == mine)
-        def _(do=do):
-            for n in range(min(EARLY), max(EARLY)):
-                for way in range(2):
-                    do(way, n)
+def each(do):
+    for way in range(2):
+        for n in range(REST):
+            do(way, n)
 
 
 def columns_of(owner):
@@ -409,19 +418,17 @@
     pl.semaphore_wait(barrier, 2)
 
     def send(way, n):
-        l, first, size = place(1 - way, n)
+        layers, first, size = stay(1 - way, n)
         return pltpu.make_async_remote_copy(
-            cc_v.at[gz, l, pl.ds(first, size), :], late_o.at[way, n, pl.ds(0, size), :],
+            cc_v.at[gz, layers, pl.ds(first, size), :], late_o.at[way, layers, pl.ds(2 * PIECE - size, size), :],
             (right_s, left_s)[way].at[n], (right_r, left_r)[way].at[n],
             device_id={"gx": gx, "gy": gy, "gz": (right, left)[way]}, device_id_type=MESH,
         )
 
-    def skip(way, n):
-        pass
-
-    core = lax.rem(gy, 2)
-    rest(core, skip, lambda way, n: send(way, n).start())
-    rest(core, skip, lambda way, n: send(way, n).wait())
+    @pl.when(lax.rem(gy, 2) == LATE_CORE)
+    def _():
+        each(lambda way, n: send(way, n).start())
+        each(lambda way, n: send(way, n).wait())
 
 
 def write_kernel(nz, np_v, rn_v, cn_v, ap_v, cc_v, np_h, rn_h, cn_h, ap_h, cc_h, sem, part_sem):
@@ -434,12 +441,18 @@
         copies[-1].start()
 
     def part(way, n):
-        l, first, size = place(1 - way, n)
+        layers, first, size = stay(1 - way, n)
         rows = pl.ds(first, size)
         owner = (left, right)[way]
         return pltpu.make_async_copy(
-            cc_v.at[owner, l, rows, :], cc_h.at[l, rows, columns_of(owner)], part_sem.at[way * PIECES + n]
-        )
+            cc_v.at[owner, layers, rows, :], cc_h.at[layers, rows, columns_of(owner)], part_sem.at[way * REST + n]
+        )
+
+    early = lax.rem(gy, 2) != LATE_CORE
+
+    @pl.when(early)
+    def _():
+        each(lambda way, n: part(way, n).start())
 
     for l in range(LAYERS):
         put(np_v.at[l], np_h.at[l])
@@ -455,14 +468,12 @@
     put(rn_v, rn_h)
     put(cn_v, cn_h)
 
-    def skip(way, n):
-        pass
-
-    core = lax.rem(gy, 2)
-    rest(core, lambda way, n: part(way, n).start(), skip)
     for copy in copies:
         copy.wait()
-    rest(core, lambda way, n: part(way, n).wait(), skip)
+
+    @pl.when(early)
+    def _():
+        each(lambda way, n: part(way, n).wait())
 
 
 def finish_kernel(nz, late_v, old_h, cc_h, part_sem):
@@ -470,18 +481,16 @@
     right, left = lax.rem(gz + 1, nz), lax.rem(gz + nz - 1, nz)
 
     def part(way, n):
-        l, first, size = place(1 - way, n)
-        rows = pl.ds(first, size)
+        layers, first, size = stay(1 - way, n)
         return pltpu.make_async_copy(
-            late_v.at[way, n, pl.ds(0, size), :], cc_h.at[l, rows, columns_of((left, right)[way])], part_sem.at[way * PIECES + n]
-        )
-
-    def skip(way, n):
-        pass
-
-    core = lax.rem(gy, 2)
-    rest(core, skip, lambda way, n: part(way, n).start())
-    rest(core, skip, lambda way, n: part(way, n).wait())
+            late_v.at[way, layers, pl.ds(2 * PIECE - size, size), :],
+            cc_h.at[layers, pl.ds(first, size), columns_of((left, right)[way])], part_sem.at[way * REST + n],
+        )
+
+    @pl.when(lax.rem(gy, 2) == LATE_CORE)
+    def _():
+        each(lambda way, n: part(way, n).start())
+        each(lambda way, n: part(way, n).wait())
 
 
 def solution(mesh):
@@ -513,6 +522,7 @@
                 V((nx * ny * nz, 1, 128), F32),
                 V((LAYERS, 8, 128), F32),
                 V((LAYERS, 1, COLS), F32),
+                V((LAYERS, 1, COLS), F32),
                 V((LAYERS, ROWS, 128), F32),
                 pltpu.SemaphoreType.REGULAR, pltpu.SemaphoreType.REGULAR,
                 sem((2 * LAYERS + 2,)),
@@ -521,8 +531,8 @@
                 sem, sem,
                 sem((nz - 1,)), sem((nz - 1,)),
                 sem((6,)), sem((6,)), sem((6,)), sem((6,)),
-                sem((3 * PIECES,)), sem((3 * PIECES,)),
-                sem((3 * PIECES,)), sem((3 * PIECES,)),
+                sem((2 * PIECES + REST,)), sem((2 * PIECES + REST,)),
+                sem((2 * PIECES + REST,)), sem((2 * PIECES + REST,)),
             ],
             compiler_params=pltpu.CompilerParams(
                 collective_id=0, has_side_effects=True, vmem_limit_bytes=16 * 2**20
@@ -539,15 +549,15 @@
             ],
             in_specs=[pl.BlockSpec(memory_space=V)] * 5,
             out_specs=[pl.BlockSpec(memory_space=pltpu.HBM)] * 5,
-            scratch_shapes=[sem((6 * LAYERS + 4,)), sem((2 * PIECES,))],
+            scratch_shapes=[sem((6 * LAYERS + 4,)), sem((2 * REST,))],
             compiler_params=pltpu.CompilerParams(vmem_limit_bytes=2**20),
         )(*kept)
         late = pl.pallas_call(
             functools.partial(rest_kernel, nz),
-            out_shape=V((2, PIECES, PIECE, COLS), BF16),
+            out_shape=V((2, LAYERS, 2 * PIECE, COLS), BF16),
             in_specs=[pl.BlockSpec(memory_space=V), pl.BlockSpec(memory_space=pltpu.HBM)],
             out_specs=pl.BlockSpec(memory_space=V),
-            scratch_shapes=[sem((PIECES,)), sem((PIECES,)), sem((PIECES,)), sem((PIECES,))],
+            scratch_shapes=[sem((REST,)), sem((REST,)), sem((REST,)), sem((REST,))],
             compiler_params=pltpu.CompilerParams(collective_id=1, has_side_effects=True, vmem_limit_bytes=2**20),
         )(kept[4], pltpu.with_memory_space_constraint(col_new, pltpu.HBM))
         compute = pl.pallas_call(
@@ -555,7 +565,7 @@
             out_shape=jax.ShapeDtypeStruct((LAYERS, ROWS, nz * COLS), BF16),
             in_specs=[pl.BlockSpec(memory_space=V), pl.BlockSpec(memory_space=pltpu.HBM)],
             out_specs=pl.BlockSpec(memory_space=pltpu.HBM),
-            scratch_shapes=[sem((2 * PIECES,))],
+            scratch_shapes=[sem((2 * REST,))],
             input_output_aliases={1: 0},
             compiler_params=pltpu.CompilerParams(vmem_limit_bytes=2**20),
         )(late, compute)

time: 88.5 us -> 87.9 us (level)
  no operation moved by 1% of the time
where the time goes in v5:
time: 87.9 us; the launch traced here: 87.8 us
  Pallas kernels  87.2 us (99%)
    pallas_call x1, Pallas kernels, body(): pl.pallas_call(functools.partial(step_kernel, (nx, ny, nz)), out_shape=[V...  65 us
    pallas_call x1, Pallas kernels, body(): pl.pallas_call(functools.partial(rest_kernel, nz), out_shape=V((2, LAYERS...  15.5 us
    pallas_call x1, Pallas kernels, body(): pl.pallas_call(functools.partial(write_kernel, nz), out_shape=[jax.ShapeD...  5.37 us

profile of v5, /device:TPU:0, one launch (start us, length us, event | category | flops | bytes accessed | tf_op | source)
XLA Modules:
  0.0 87.8 jit_solution(9834614614624585645)
XLA Ops:
  0.6 65.0 %shard_map.83 = (f32[3,896,384]{2,1,0:T(8,128)S(1)}, f32[3,896]{1,0:T(4,128)S(1)}, f32[3,384]{1,0:T(4,128)S(1)}, f32[3,896,384]{2,1,0:T(8,128)S(1)}, bf16[4,3,896,384]{3,2,1,0:T(8,128)(2,1)S(1)}) custom-call(f32[3,896,384]{2,1,0:T(8,128)} %p_h.1, bf16[3,896,384]{2,1,0:T(8,128)(2,1)} %g_h.1, f32[3,896]{1,0:T(4,128)} %rs_h.1, f32[3,384]{1,0:T(4,128)} %cs_h.1), custom_call_target="tpu_custom_call" | custom-call | tf_op jit(solution)/shard_map/pallas_call | solution.py:502
  65.6 5.4 %shard_map.84 = (f32[3,896,384]{2,1,0:T(8,128)}, f32[3,896]{1,0:T(4,128)}, f32[3,384]{1,0:T(4,128)}, f32[3,896,384]{2,1,0:T(8,128)}, bf16[3,896,1536]{2,1,0:T(8,128)(2,1)}) custom-call(f32[3,896,384]{2,1,0:T(8,128)S(1)} %get-tuple-element.15.np_v, f32[3,896]{1,0:T(4,128)S(1)} %get-tuple-element.16.rn_v, f32[3,384]{1,0:T(4,128)S(1)} %get-tuple-element.17.cn_v, ...), custom_call_target="tpu_custom_call" | custom-call | tf_op jit(solution)/shard_map/pallas_call | solution.py:541
  71.0 15.5 %shard_map.85.late_v = bf16[2,3,448,384]{3,2,1,0:T(8,128)(2,1)S(1)} custom-call(bf16[4,3,896,384]{3,2,1,0:T(8,128)(2,1)S(1)} %get-tuple-element.19.cc_v, f32[3,384]{1,0:T(4,128)} %get-tuple-element.12.after_h), custom_call_target="tpu_custom_call" | custom-call | tf_op jit(solution)/shard_map/pallas_call | solution.py:555
  86.5 1.3 %shard_map.86 = bf16[3,896,1536]{2,1,0:T(8,128)(2,1)} custom-call(bf16[2,3,448,384]{3,2,1,0:T(8,128)(2,1)S(1)} %shard_map.85.late_v, bf16[3,896,1536]{2,1,0:T(8,128)(2,1)} %get-tuple-element.24.old_h), custom_call_target="tpu_custom_call", output_to_operand_aliasing={{}: (1, {})} | custom-call | tf_op jit(solution)/shard_map/pallas_call | solution.py:563

commit v6 on v5

--- a/solution.py
+++ b/solution.py
@@ -24,7 +24,7 @@
 PIECE = ROWS // 4
 PIECES = 2 * LAYERS
 REST = 2
-LATE_CORE = 0
+LATE_CORE = 1
 
 
 def place(kind, n):

time: 87.9 us -> 86.9 us (0.989)
  the two profiles are of different devices: /device:TPU:0 before, /device:TPU:1 now
where the time goes in v6:
time: 86.9 us; the launch traced here: 86.8 us
  Pallas kernels  86.1 us (99%)
    pallas_call x1, Pallas kernels, body(): pl.pallas_call(functools.partial(step_kernel, (nx, ny, nz)), out_shape=[V...  64.3 us
    pallas_call x1, Pallas kernels, body(): pl.pallas_call(functools.partial(rest_kernel, nz), out_shape=V((2, LAYERS...  15.2 us
    pallas_call x1, Pallas kernels, body(): pl.pallas_call(functools.partial(write_kernel, nz), out_shape=[jax.ShapeD...  5.37 us

profile of v6, /device:TPU:1, one launch (start us, length us, event | category | flops | bytes accessed | tf_op | source)
XLA Modules:
  0.0 86.8 jit_solution(16003615521997136527)
XLA Ops:
  0.6 64.3 %shard_map.83 = (f32[3,896,384]{2,1,0:T(8,128)S(1)}, f32[3,896]{1,0:T(4,128)S(1)}, f32[3,384]{1,0:T(4,128)S(1)}, f32[3,896,384]{2,1,0:T(8,128)S(1)}, bf16[4,3,896,384]{3,2,1,0:T(8,128)(2,1)S(1)}) custom-call(f32[3,896,384]{2,1,0:T(8,128)} %p_h.1, bf16[3,896,384]{2,1,0:T(8,128)(2,1)} %g_h.1, f32[3,896]{1,0:T(4,128)} %rs_h.1, f32[3,384]{1,0:T(4,128)} %cs_h.1), custom_call_target="tpu_custom_call" | custom-call | tf_op jit(solution)/shard_map/pallas_call | solution.py:502
  64.9 5.4 %shard_map.84 = (f32[3,896,384]{2,1,0:T(8,128)}, f32[3,896]{1,0:T(4,128)}, f32[3,384]{1,0:T(4,128)}, f32[3,896,384]{2,1,0:T(8,128)}, bf16[3,896,1536]{2,1,0:T(8,128)(2,1)}) custom-call(f32[3,896,384]{2,1,0:T(8,128)S(1)} %get-tuple-element.15.np_v, f32[3,896]{1,0:T(4,128)S(1)} %get-tuple-element.16.rn_v, f32[3,384]{1,0:T(4,128)S(1)} %get-tuple-element.17.cn_v, ...), custom_call_target="tpu_custom_call" | custom-call | tf_op jit(solution)/shard_map/pallas_call | solution.py:541
  70.3 15.2 %shard_map.85.late_v = bf16[2,3,448,384]{3,2,1,0:T(8,128)(2,1)S(1)} custom-call(bf16[4,3,896,384]{3,2,1,0:T(8,128)(2,1)S(1)} %get-tuple-element.19.cc_v, f32[3,384]{1,0:T(4,128)} %get-tuple-element.12.after_h), custom_call_target="tpu_custom_call" | custom-call | tf_op jit(solution)/shard_map/pallas_call | solution.py:555
  85.5 1.3 %shard_map.86 = bf16[3,896,1536]{2,1,0:T(8,128)(2,1)} custom-call(bf16[2,3,448,384]{3,2,1,0:T(8,128)(2,1)S(1)} %shard_map.85.late_v, bf16[3,896,1536]{2,1,0:T(8,128)(2,1)} %get-tuple-element.24.old_h), custom_call_target="tpu_custom_call", output_to_operand_aliasing={{}: (1, {})} | custom-call | tf_op jit(solution)/shard_map/pallas_call | solution.py:563

commit v7 on v6

--- a/solution.py
+++ b/solution.py
@@ -20,7 +20,7 @@
 ROWS = 896
 COLS = 384
 STEP = 112
-RAW = 64
+RAW = 80
 PIECE = ROWS // 4
 PIECES = 2 * LAYERS
 REST = 2
@@ -191,6 +191,14 @@
     for pair in raws[0]:
         for copy in pair:
             copy.start()
+    near = jnp.logical_and(gx == 0, gy // 2 == 0)
+
+    @pl.when(near)
+    def _():
+        for pair in raws[1]:
+            for copy in pair:
+                copy.start()
+
 
     row1 = lanes((1, 128))
 
@@ -276,9 +284,12 @@
         ).start()
     for copy in inverse:
         copy.start()
-    for pair in raws[1]:
-        for copy in pair:
-            copy.start()
+    @pl.when(jnp.logical_not(near))
+    def _():
+        for pair in raws[1]:
+            for copy in pair:
+                copy.start()
+
     for way in range(2):
         for copy in raws[0][way]:
             copy.wait_recv()

time: 86.9 us -> 86.4 us (level)
  no operation moved by 1% of the time
where the time goes in v7:
time: 86.4 us; the launch traced here: 86.3 us
  Pallas kernels  85.7 us (99%)
    pallas_call x1, Pallas kernels, body(): pl.pallas_call(functools.partial(step_kernel, (nx, ny, nz)), out_shape=[V...  64.4 us
    pallas_call x1, Pallas kernels, body(): pl.pallas_call(functools.partial(rest_kernel, nz), out_shape=V((2, LAYERS...  14.6 us
    pallas_call x1, Pallas kernels, body(): pl.pallas_call(functools.partial(write_kernel, nz), out_shape=[jax.ShapeD...  5.38 us

profile of v7, /device:TPU:1, one launch (start us, length us, event | category | flops | bytes accessed | tf_op | source)
XLA Modules:
  0.0 86.3 jit_solution(4771156822648208997)
XLA Ops:
  0.6 64.4 %shard_map.83 = (f32[3,896,384]{2,1,0:T(8,128)S(1)}, f32[3,896]{1,0:T(4,128)S(1)}, f32[3,384]{1,0:T(4,128)S(1)}, f32[3,896,384]{2,1,0:T(8,128)S(1)}, bf16[4,3,896,384]{3,2,1,0:T(8,128)(2,1)S(1)}) custom-call(f32[3,896,384]{2,1,0:T(8,128)} %p_h.1, bf16[3,896,384]{2,1,0:T(8,128)(2,1)} %g_h.1, f32[3,896]{1,0:T(4,128)} %rs_h.1, f32[3,384]{1,0:T(4,128)} %cs_h.1), custom_call_target="tpu_custom_call" | custom-call | tf_op jit(solution)/shard_map/pallas_call | solution.py:513
  65.0 5.4 %shard_map.84 = (f32[3,896,384]{2,1,0:T(8,128)}, f32[3,896]{1,0:T(4,128)}, f32[3,384]{1,0:T(4,128)}, f32[3,896,384]{2,1,0:T(8,128)}, bf16[3,896,1536]{2,1,0:T(8,128)(2,1)}) custom-call(f32[3,896,384]{2,1,0:T(8,128)S(1)} %get-tuple-element.15.np_v, f32[3,896]{1,0:T(4,128)S(1)} %get-tuple-element.16.rn_v, f32[3,384]{1,0:T(4,128)S(1)} %get-tuple-element.17.cn_v, ...), custom_call_target="tpu_custom_call" | custom-call | tf_op jit(solution)/shard_map/pallas_call | solution.py:552
  70.4 14.6 %shard_map.85.late_v = bf16[2,3,448,384]{3,2,1,0:T(8,128)(2,1)S(1)} custom-call(bf16[4,3,896,384]{3,2,1,0:T(8,128)(2,1)S(1)} %get-tuple-element.19.cc_v, f32[3,384]{1,0:T(4,128)} %get-tuple-element.12.after_h), custom_call_target="tpu_custom_call" | custom-call | tf_op jit(solution)/shard_map/pallas_call | solution.py:566
  85.0 1.3 %shard_map.86 = bf16[3,896,1536]{2,1,0:T(8,128)(2,1)} custom-call(bf16[2,3,448,384]{3,2,1,0:T(8,128)(2,1)S(1)} %shard_map.85.late_v, bf16[3,896,1536]{2,1,0:T(8,128)(2,1)} %get-tuple-element.24.old_h), custom_call_target="tpu_custom_call", output_to_operand_aliasing={{}: (1, {})} | custom-call | tf_op jit(solution)/shard_map/pallas_call | solution.py:574

commit v8 on v7

--- a/solution.py
+++ b/solution.py
@@ -269,8 +269,8 @@
         for i in range(1, nz)
     ]
 
+    all_x[(gx * ny + gy) * nz + gz] = payload
     pl.semaphore_wait(told_plane, len(line_y))
-    all_x[(gx * ny + gy) * nz + gz] = payload
     mine = all_x.at[(gx * ny + gy) * nz + gz]
 
     def far(at):

time: 86.4 us -> 86.4 us (level)
  no operation moved by 1% of the time
where the time goes in v8:
time: 86.4 us; the launch traced here: 86.3 us
  Pallas kernels  85.7 us (99%)
    pallas_call x1, Pallas kernels, body(): pl.pallas_call(functools.partial(step_kernel, (nx, ny, nz)), out_shape=[V...  64.4 us
    pallas_call x1, Pallas kernels, body(): pl.pallas_call(functools.partial(rest_kernel, nz), out_shape=V((2, LAYERS...  14.6 us
    pallas_call x1, Pallas kernels, body(): pl.pallas_call(functools.partial(write_kernel, nz), out_shape=[jax.ShapeD...  5.38 us

profile of v8, /device:TPU:1, one launch (start us, length us, event | category | flops | bytes accessed | tf_op | source)
XLA Modules:
  0.0 86.3 jit_solution(2992252434409451936)
XLA Ops:
  0.6 64.4 %shard_map.83 = (f32[3,896,384]{2,1,0:T(8,128)S(1)}, f32[3,896]{1,0:T(4,128)S(1)}, f32[3,384]{1,0:T(4,128)S(1)}, f32[3,896,384]{2,1,0:T(8,128)S(1)}, bf16[4,3,896,384]{3,2,1,0:T(8,128)(2,1)S(1)}) custom-call(f32[3,896,384]{2,1,0:T(8,128)} %p_h.1, bf16[3,896,384]{2,1,0:T(8,128)(2,1)} %g_h.1, f32[3,896]{1,0:T(4,128)} %rs_h.1, f32[3,384]{1,0:T(4,128)} %cs_h.1), custom_call_target="tpu_custom_call" | custom-call | tf_op jit(solution)/shard_map/pallas_call | solution.py:513
  65.0 5.4 %shard_map.84 = (f32[3,896,384]{2,1,0:T(8,128)}, f32[3,896]{1,0:T(4,128)}, f32[3,384]{1,0:T(4,128)}, f32[3,896,384]{2,1,0:T(8,128)}, bf16[3,896,1536]{2,1,0:T(8,128)(2,1)}) custom-call(f32[3,896,384]{2,1,0:T(8,128)S(1)} %get-tuple-element.15.np_v, f32[3,896]{1,0:T(4,128)S(1)} %get-tuple-element.16.rn_v, f32[3,384]{1,0:T(4,128)S(1)} %get-tuple-element.17.cn_v, ...), custom_call_target="tpu_custom_call" | custom-call | tf_op jit(solution)/shard_map/pallas_call | solution.py:552
  70.4 14.6 %shard_map.85.late_v = bf16[2,3,448,384]{3,2,1,0:T(8,128)(2,1)S(1)} custom-call(bf16[4,3,896,384]{3,2,1,0:T(8,128)(2,1)S(1)} %get-tuple-element.19.cc_v, f32[3,384]{1,0:T(4,128)} %get-tuple-element.12.after_h), custom_call_target="tpu_custom_call" | custom-call | tf_op jit(solution)/shard_map/pallas_call | solution.py:566
  85.0 1.3 %shard_map.86 = bf16[3,896,1536]{2,1,0:T(8,128)(2,1)} custom-call(bf16[2,3,448,384]{3,2,1,0:T(8,128)(2,1)S(1)} %shard_map.85.late_v, bf16[3,896,1536]{2,1,0:T(8,128)(2,1)} %get-tuple-element.24.old_h), custom_call_target="tpu_custom_call", output_to_operand_aliasing={{}: (1, {})} | custom-call | tf_op jit(solution)/shard_map/pallas_call | solution.py:574
